TPU v7x, 8 devices: a whole 2x2x1 slice. The times are simulated.
8 devices in a mesh: col: 4 (over z, y, x), row: 2 (over core).
Axes of the slice: x: 2, y: 2, z: 1, core: 2. Of those that a mesh axis runs over, the one named last changes fastest.
Arguments:
- trans_mat: bfloat16 [24576, 24576], P('row', 'col')
- x_start: float32 [24576, 256], P(('col', 'row'))
- teleport: float32 [24576, 256], P(('col', 'row'))
- dangling: int32 [24576], P(('col', 'row'))
Outputs:
- output: float32 [24576, 256], P(('col', 'row'))
All inputs are finite; a program needn't handle non-finite values.
Results may differ from a plain program's by a relative error of at most 0.001.
Values are sent between devices in bfloat16 or wider.
A program may use at most 1 GiB of HBM per device.

v0:
```python
import jax
import jax.numpy as jnp
from jax import lax
from jax.sharding import PartitionSpec as P

SWEEPS = 8
DAMPING = 0.85


def solution(mesh):
    row_size = mesh.shape['row']
    col_size = mesh.shape['col']
    realign = [(col_idx * row_size + row_idx, row_idx * col_size + col_idx)
               for row_idx in range(row_size) for col_idx in range(col_size)]

    def local_sweeps(mat_tile, x_piece, tele_piece, dang_piece):
        vertex_count = mat_tile.shape[1] * col_size
        dang_col = dang_piece.astype(jnp.float32)[:, None]
        x_cur = x_piece
        for sweep_idx in range(SWEEPS):
            dang_mass = lax.psum(jnp.sum(dang_col * x_cur, axis=0), ('col', 'row')) / vertex_count
            x_src = lax.all_gather(x_cur.astype(jnp.bfloat16), 'row', axis=0, tiled=True)
            part_prod = jnp.dot(mat_tile, x_src, preferred_element_type=jnp.float32)
            folded = lax.psum_scatter(part_prod, 'col', scatter_dimension=0, tiled=True)
            aligned = lax.ppermute(folded, ('col', 'row'), perm=realign)
            x_cur = DAMPING * aligned + (DAMPING * dang_mass + (1.0 - DAMPING))[None, :] * tele_piece
        return x_cur

    vec_spec = P(('col', 'row'), None)
    return jax.shard_map(local_sweeps, mesh=mesh,
                         in_specs=(P('row', 'col'), vec_spec, vec_spec, P(('col', 'row'))),
                         out_specs=vec_spec, check_vma=False)
```

profile of v0, /device:TPU:0, one launch (start us, length us, event | category | flops | bytes accessed | tf_op | source)
XLA Modules:
  0.0 2254.1 jit_solution(1053699985061530889)
XLA Ops:
  24.4 59.1 %fusion.8 = f32[12288,256]{1,0:T(8,128)} fusion(bf16[12288,6144]{1,0:T(8,128)(2,1)} %param.4, bf16[6144,256]{1,0:T(8,128)(2,1)} %all-gather.9.cloned.1.call-done), kind=kOutput, calls=%fused_computation.39 | convolution fusion | flops 38654705664 | bytes 166723584 | tf_op jit(solution)/shard_map/dot_general | solution.py:23
  83.5 116.1 %reduce-scatter.9.cloned.1.call-done = f32[3072,256]{1,0:T(8,128)} async-done(((f32[12288,256]{1,0:T(8,128)}), f32[3072,256]{1,0:T(8,128)}) %reduce-scatter.9.cloned.1.call-update) | async-done | bytes 3145744 | tf_op jit(solution)/shard_map/reduce_scatter | solution.py:24
  199.6 25.0 %collective-permute-start = (f32[3072,256]{1,0:T(8,128)}, f32[3072,256]{1,0:T(8,128)}, u32[]{:S(2)}, u32[]{:S(2)}) collective-permute-start(f32[3072,256]{1,0:T(8,128)} %reduce-scatter.9.cloned.1.call-done), channel_id=1, source_target_pairs={{0,0},{2,1},{4,2},{6,3},{1,4},{3,5},{5,6},{7,7}} | collective-permute-start | bytes 9437192 | tf_op jit(solution)/shard_map/ppermute | solution.py:25
  224.6 64.6 %psum.56 = f32[256]{0:T(256)S(1)} all-reduce(f32[256]{0:T(256)S(1)} %get-tuple-element.20), channel_id=1, replica_groups=mesh['col'=4,'row'=2] {'col','row'}, use_global_device_ids=true, to_apply=%region_2.0 | all-reduce | flops 256 | bytes 2048 | tf_op jit(solution)/shard_map/psum | solution.py:21
  303.5 59.1 %convolution_bitcast_fusion.6 = f32[12288,256]{1,0:T(8,128)} fusion(bf16[12288,6144]{1,0:T(8,128)(2,1)} %param.4, bf16[6144,256]{1,0:T(8,128)(2,1)} %all-gather.11.cloned.1.call-done), kind=kOutput, calls=%fused_computation.6 | convolution fusion | flops 38654705664 | bytes 166723584 | tf_op jit(solution)/shard_map/dot_general | solution.py:23
  362.7 116.1 %reduce-scatter.11.cloned.1.call-done = f32[3072,256]{1,0:T(8,128)} async-done(((f32[12288,256]{1,0:T(8,128)}), f32[3072,256]{1,0:T(8,128)}) %reduce-scatter.11.cloned.1.call-update) | async-done | bytes 3145744 | tf_op jit(solution)/shard_map/reduce_scatter | solution.py:24
  478.8 25.0 %collective-permute-start.1 = (f32[3072,256]{1,0:T(8,128)}, f32[3072,256]{1,0:T(8,128)}, u32[]{:S(2)}, u32[]{:S(2)}) collective-permute-start(f32[3072,256]{1,0:T(8,128)} %reduce-scatter.11.cloned.1.call-done), channel_id=1, source_target_pairs={{0,0},{2,1},{4,2},{6,3},{1,4},{3,5},{5,6},{7,7}} | collective-permute-start | bytes 9437192 | tf_op jit(solution)/shard_map/ppermute | solution.py:25
  503.8 64.6 %psum.57 = f32[256]{0:T(256)S(1)} all-reduce(f32[256]{0:T(256)S(1)} %get-tuple-element.18), channel_id=1, replica_groups=mesh['col'=4,'row'=2] {'col','row'}, use_global_device_ids=true, to_apply=%region_5.0 | all-reduce | flops 256 | bytes 2048 | tf_op jit(solution)/shard_map/psum | solution.py:21
  582.7 59.1 %convolution_bitcast_fusion.5 = f32[12288,256]{1,0:T(8,128)} fusion(bf16[12288,6144]{1,0:T(8,128)(2,1)} %param.4, bf16[6144,256]{1,0:T(8,128)(2,1)} %all-gather.13.cloned.1.call-done), kind=kOutput, calls=%fused_computation.5 | convolution fusion | flops 38654705664 | bytes 166723584 | tf_op jit(solution)/shard_map/dot_general | solution.py:23
  641.8 116.1 %reduce-scatter.13.cloned.1.call-done = f32[3072,256]{1,0:T(8,128)} async-done(((f32[12288,256]{1,0:T(8,128)}), f32[3072,256]{1,0:T(8,128)}) %reduce-scatter.13.cloned.1.call-update) | async-done | bytes 3145744 | tf_op jit(solution)/shard_map/reduce_scatter | solution.py:24
  757.9 25.0 %collective-permute-start.2 = (f32[3072,256]{1,0:T(8,128)}, f32[3072,256]{1,0:T(8,128)}, u32[]{:S(2)}, u32[]{:S(2)}) collective-permute-start(f32[3072,256]{1,0:T(8,128)} %reduce-scatter.13.cloned.1.call-done), channel_id=1, source_target_pairs={{0,0},{2,1},{4,2},{6,3},{1,4},{3,5},{5,6},{7,7}} | collective-permute-start | bytes 9437192 | tf_op jit(solution)/shard_map/ppermute | solution.py:25
  782.9 64.6 %psum.58 = f32[256]{0:T(256)S(1)} all-reduce(f32[256]{0:T(256)S(1)} %get-tuple-element.16), channel_id=1, replica_groups=mesh['col'=4,'row'=2] {'col','row'}, use_global_device_ids=true, to_apply=%region_8.0 | all-reduce | flops 256 | bytes 2048 | tf_op jit(solution)/shard_map/psum | solution.py:21
  861.8 59.1 %convolution_bitcast_fusion.4 = f32[12288,256]{1,0:T(8,128)} fusion(bf16[12288,6144]{1,0:T(8,128)(2,1)} %param.4, bf16[6144,256]{1,0:T(8,128)(2,1)} %all-gather.15.cloned.1.call-done), kind=kOutput, calls=%fused_computation.4 | convolution fusion | flops 38654705664 | bytes 166723584 | tf_op jit(solution)/shard_map/dot_general | solution.py:23
  920.9 116.1 %reduce-scatter.15.cloned.1.call-done = f32[3072,256]{1,0:T(8,128)} async-done(((f32[12288,256]{1,0:T(8,128)}), f32[3072,256]{1,0:T(8,128)}) %reduce-scatter.15.cloned.1.call-update) | async-done | bytes 3145744 | tf_op jit(solution)/shard_map/reduce_scatter | solution.py:24
  1037.0 25.0 %collective-permute-start.3 = (f32[3072,256]{1,0:T(8,128)}, f32[3072,256]{1,0:T(8,128)}, u32[]{:S(2)}, u32[]{:S(2)}) collective-permute-start(f32[3072,256]{1,0:T(8,128)} %reduce-scatter.15.cloned.1.call-done), channel_id=1, source_target_pairs={{0,0},{2,1},{4,2},{6,3},{1,4},{3,5},{5,6},{7,7}} | collective-permute-start | bytes 9437192 | tf_op jit(solution)/shard_map/ppermute | solution.py:25
  1062.0 64.6 %psum.59 = f32[256]{0:T(256)S(1)} all-reduce(f32[256]{0:T(256)S(1)} %get-tuple-element.14), channel_id=1, replica_groups=mesh['col'=4,'row'=2] {'col','row'}, use_global_device_ids=true, to_apply=%region_11.0 | all-reduce | flops 256 | bytes 2048 | tf_op jit(solution)/shard_map/psum | solution.py:21
  1140.9 59.1 %convolution_bitcast_fusion.3 = f32[12288,256]{1,0:T(8,128)} fusion(bf16[12288,6144]{1,0:T(8,128)(2,1)} %param.4, bf16[6144,256]{1,0:T(8,128)(2,1)} %all-gather.17.cloned.1.call-done), kind=kOutput, calls=%fused_computation.3 | convolution fusion | flops 38654705664 | bytes 166723584 | tf_op jit(solution)/shard_map/dot_general | solution.py:23
  1200.0 116.1 %reduce-scatter.17.cloned.1.call-done = f32[3072,256]{1,0:T(8,128)} async-done(((f32[12288,256]{1,0:T(8,128)}), f32[3072,256]{1,0:T(8,128)}) %reduce-scatter.17.cloned.1.call-update) | async-done | bytes 3145744 | tf_op jit(solution)/shard_map/reduce_scatter | solution.py:24
  1316.2 25.0 %collective-permute-start.4 = (f32[3072,256]{1,0:T(8,128)}, f32[3072,256]{1,0:T(8,128)}, u32[]{:S(2)}, u32[]{:S(2)}) collective-permute-start(f32[3072,256]{1,0:T(8,128)} %reduce-scatter.17.cloned.1.call-done), channel_id=1, source_target_pairs={{0,0},{2,1},{4,2},{6,3},{1,4},{3,5},{5,6},{7,7}} | collective-permute-start | bytes 9437192 | tf_op jit(solution)/shard_map/ppermute | solution.py:25
  1341.2 64.6 %psum.60 = f32[256]{0:T(256)S(1)} all-reduce(f32[256]{0:T(256)S(1)} %get-tuple-element.12), channel_id=1, replica_groups=mesh['col'=4,'row'=2] {'col','row'}, use_global_device_ids=true, to_apply=%region_14.0 | all-reduce | flops 256 | bytes 2048 | tf_op jit(solution)/shard_map/psum | solution.py:21
  1420.1 59.1 %convolution_bitcast_fusion.2 = f32[12288,256]{1,0:T(8,128)} fusion(bf16[12288,6144]{1,0:T(8,128)(2,1)} %param.4, bf16[6144,256]{1,0:T(8,128)(2,1)} %all-gather.19.cloned.1.call-done), kind=kOutput, calls=%fused_computation.2 | convolution fusion | flops 38654705664 | bytes 166723584 | tf_op jit(solution)/shard_map/dot_general | solution.py:23
  1479.2 116.1 %reduce-scatter.19.cloned.1.call-done = f32[3072,256]{1,0:T(8,128)} async-done(((f32[12288,256]{1,0:T(8,128)}), f32[3072,256]{1,0:T(8,128)}) %reduce-scatter.19.cloned.1.call-update) | async-done | bytes 3145744 | tf_op jit(solution)/shard_map/reduce_scatter | solution.py:24
  1595.3 25.0 %collective-permute-start.5 = (f32[3072,256]{1,0:T(8,128)}, f32[3072,256]{1,0:T(8,128)}, u32[]{:S(2)}, u32[]{:S(2)}) collective-permute-start(f32[3072,256]{1,0:T(8,128)} %reduce-scatter.19.cloned.1.call-done), channel_id=1, source_target_pairs={{0,0},{2,1},{4,2},{6,3},{1,4},{3,5},{5,6},{7,7}} | collective-permute-start | bytes 9437192 | tf_op jit(solution)/shard_map/ppermute | solution.py:25
  1620.3 64.6 %psum.61 = f32[256]{0:T(256)S(1)} all-reduce(f32[256]{0:T(256)S(1)} %get-tuple-element.10), channel_id=1, replica_groups=mesh['col'=4,'row'=2] {'col','row'}, use_global_device_ids=true, to_apply=%region_17.0 | all-reduce | flops 256 | bytes 2048 | tf_op jit(solution)/shard_map/psum | solution.py:21
  1699.2 59.1 %convolution_bitcast_fusion.1 = f32[12288,256]{1,0:T(8,128)} fusion(bf16[12288,6144]{1,0:T(8,128)(2,1)} %param.4, bf16[6144,256]{1,0:T(8,128)(2,1)} %all-gather.21.cloned.1.call-done), kind=kOutput, calls=%fused_computation.1 | convolution fusion | flops 38654705664 | bytes 166723584 | tf_op jit(solution)/shard_map/dot_general | solution.py:23
  1758.3 116.1 %reduce-scatter.21.cloned.1.call-done = f32[3072,256]{1,0:T(8,128)} async-done(((f32[12288,256]{1,0:T(8,128)}), f32[3072,256]{1,0:T(8,128)}) %reduce-scatter.21.cloned.1.call-update) | async-done | bytes 3145744 | tf_op jit(solution)/shard_map/reduce_scatter | solution.py:24
  1874.4 25.0 %collective-permute-start.6 = (f32[3072,256]{1,0:T(8,128)}, f32[3072,256]{1,0:T(8,128)}, u32[]{:S(2)}, u32[]{:S(2)}) collective-permute-start(f32[3072,256]{1,0:T(8,128)} %reduce-scatter.21.cloned.1.call-done), channel_id=1, source_target_pairs={{0,0},{2,1},{4,2},{6,3},{1,4},{3,5},{5,6},{7,7}} | collective-permute-start | bytes 9437192 | tf_op jit(solution)/shard_map/ppermute | solution.py:25
  1899.4 64.6 %psum.62 = f32[256]{0:T(256)S(1)} all-reduce(f32[256]{0:T(256)S(1)} %get-tuple-element.8), channel_id=1, replica_groups=mesh['col'=4,'row'=2] {'col','row'}, use_global_device_ids=true, to_apply=%region_20.0 | all-reduce | flops 256 | bytes 2048 | tf_op jit(solution)/shard_map/psum | solution.py:21
  1978.3 59.1 %convolution_bitcast_fusion = f32[12288,256]{1,0:T(8,128)} fusion(bf16[12288,6144]{1,0:T(8,128)(2,1)} %param.4, bf16[6144,256]{1,0:T(8,128)(2,1)} %all-gather.23.cloned.1.call-done), kind=kOutput, calls=%fused_computation | convolution fusion | flops 38654705664 | bytes 166723584 | tf_op jit(solution)/shard_map/dot_general | solution.py:23
  2037.4 116.1 %reduce-scatter.23.cloned.1.call-done = f32[3072,256]{1,0:T(8,128)} async-done(((f32[12288,256]{1,0:T(8,128)}), f32[3072,256]{1,0:T(8,128)}) %reduce-scatter.23.cloned.1.call-update) | async-done | bytes 3145744 | tf_op jit(solution)/shard_map/reduce_scatter | solution.py:24
  2153.6 25.0 %collective-permute-start.7 = (f32[3072,256]{1,0:T(8,128)}, f32[3072,256]{1,0:T(8,128)}, u32[]{:S(2)}, u32[]{:S(2)}) collective-permute-start(f32[3072,256]{1,0:T(8,128)} %reduce-scatter.23.cloned.1.call-done), channel_id=1, source_target_pairs={{0,0},{2,1},{4,2},{6,3},{1,4},{3,5},{5,6},{7,7}} | collective-permute-start | bytes 9437192 | tf_op jit(solution)/shard_map/ppermute | solution.py:25
  2178.5 64.6 %psum.63 = f32[256]{0:T(256)S(1)} all-reduce(f32[256]{0:T(256)S(1)} %get-tuple-element.5), channel_id=1, replica_groups=mesh['col'=4,'row'=2] {'col','row'}, use_global_device_ids=true, to_apply=%region_23.0 | all-reduce | flops 256 | bytes 2048 | tf_op jit(solution)/shard_map/psum | solution.py:21
  (68 shorter events, 122.2 us)
Async XLA Ops:
  6.5 17.9 all-gather.9.cloned.1.call-start
  11.9 187.8 %reduce-scatter.9.cloned.1.call-start = ((), (), s32[]{:S(2)}) async-start(), calls=%async_computation.9 | async-start | bytes 15728640 | tf_op jit(solution)/shard_map/reduce_scatter | solution.py:24
  83.4 205.8 %copy-start = (f32[3072,256]{1,0:T(8,128)S(1)}, f32[3072,256]{1,0:T(8,128)}, u32[]{:S(2)}) copy-start(f32[3072,256]{1,0:T(8,128)} %param.6) | copy-start | bytes 9437188
  83.5 220.1 %all-gather.11.cloned.1.call-start = ((), (), s32[]{:S(2)}) async-start(), calls=%async_computation.10 | async-start | bytes 4718592 | tf_op jit(solution)/shard_map/all_gather | solution.py:22
  199.6 89.6 %collective-permute-start = (f32[3072,256]{1,0:T(8,128)}, f32[3072,256]{1,0:T(8,128)}, u32[]{:S(2)}, u32[]{:S(2)}) collective-permute-start(f32[3072,256]{1,0:T(8,128)} %reduce-scatter.9.cloned.1.call-done), channel_id=1, source_target_pairs={{0,0},{2,1},{4,2},{6,3},{1,4},{3,5},{5,6},{7,7}} | collective-permute-start | bytes 9437192 | tf_op jit(solution)/shard_map/ppermute | solution.py:25
  292.9 185.9 %reduce-scatter.11.cloned.1.call-start = ((), (), s32[]{:S(2)}) async-start(), calls=%async_computation.11 | async-start | bytes 15728640 | tf_op jit(solution)/shard_map/reduce_scatter | solution.py:24
  362.6 220.1 %all-gather.13.cloned.1.call-start = ((), (), s32[]{:S(2)}) async-start(), calls=%async_computation.12 | async-start | bytes 4718592 | tf_op jit(solution)/shard_map/all_gather | solution.py:22
  478.8 89.6 %collective-permute-start.1 = (f32[3072,256]{1,0:T(8,128)}, f32[3072,256]{1,0:T(8,128)}, u32[]{:S(2)}, u32[]{:S(2)}) collective-permute-start(f32[3072,256]{1,0:T(8,128)} %reduce-scatter.11.cloned.1.call-done), channel_id=1, source_target_pairs={{0,0},{2,1},{4,2},{6,3},{1,4},{3,5},{5,6},{7,7}} | collective-permute-start | bytes 9437192 | tf_op jit(solution)/shard_map/ppermute | solution.py:25
  572.0 185.9 %reduce-scatter.13.cloned.1.call-start = ((), (), s32[]{:S(2)}) async-start(), calls=%async_computation.13 | async-start | bytes 15728640 | tf_op jit(solution)/shard_map/reduce_scatter | solution.py:24
  641.8 220.0 %all-gather.15.cloned.1.call-start = ((), (), s32[]{:S(2)}) async-start(), calls=%async_computation.14 | async-start | bytes 4718592 | tf_op jit(solution)/shard_map/all_gather | solution.py:22
  757.9 89.6 %collective-permute-start.2 = (f32[3072,256]{1,0:T(8,128)}, f32[3072,256]{1,0:T(8,128)}, u32[]{:S(2)}, u32[]{:S(2)}) collective-permute-start(f32[3072,256]{1,0:T(8,128)} %reduce-scatter.13.cloned.1.call-done), channel_id=1, source_target_pairs={{0,0},{2,1},{4,2},{6,3},{1,4},{3,5},{5,6},{7,7}} | collective-permute-start | bytes 9437192 | tf_op jit(solution)/shard_map/ppermute | solution.py:25
  851.1 185.9 %reduce-scatter.15.cloned.1.call-start = ((), (), s32[]{:S(2)}) async-start(), calls=%async_computation.15 | async-start | bytes 15728640 | tf_op jit(solution)/shard_map/reduce_scatter | solution.py:24
  920.9 220.0 %all-gather.17.cloned.1.call-start = ((), (), s32[]{:S(2)}) async-start(), calls=%async_computation.16 | async-start | bytes 4718592 | tf_op jit(solution)/shard_map/all_gather | solution.py:22
  1037.0 89.6 %collective-permute-start.3 = (f32[3072,256]{1,0:T(8,128)}, f32[3072,256]{1,0:T(8,128)}, u32[]{:S(2)}, u32[]{:S(2)}) collective-permute-start(f32[3072,256]{1,0:T(8,128)} %reduce-scatter.15.cloned.1.call-done), channel_id=1, source_target_pairs={{0,0},{2,1},{4,2},{6,3},{1,4},{3,5},{5,6},{7,7}} | collective-permute-start | bytes 9437192 | tf_op jit(solution)/shard_map/ppermute | solution.py:25
  1130.3 185.9 %reduce-scatter.17.cloned.1.call-start = ((), (), s32[]{:S(2)}) async-start(), calls=%async_computation.17 | async-start | bytes 15728640 | tf_op jit(solution)/shard_map/reduce_scatter | solution.py:24
  1200.0 220.1 %all-gather.19.cloned.1.call-start = ((), (), s32[]{:S(2)}) async-start(), calls=%async_computation.18 | async-start | bytes 4718592 | tf_op jit(solution)/shard_map/all_gather | solution.py:22
  1316.2 89.6 %collective-permute-start.4 = (f32[3072,256]{1,0:T(8,128)}, f32[3072,256]{1,0:T(8,128)}, u32[]{:S(2)}, u32[]{:S(2)}) collective-permute-start(f32[3072,256]{1,0:T(8,128)} %reduce-scatter.17.cloned.1.call-done), channel_id=1, source_target_pairs={{0,0},{2,1},{4,2},{6,3},{1,4},{3,5},{5,6},{7,7}} | collective-permute-start | bytes 9437192 | tf_op jit(solution)/shard_map/ppermute | solution.py:25
  1409.4 185.9 %reduce-scatter.19.cloned.1.call-start = ((), (), s32[]{:S(2)}) async-start(), calls=%async_computation.19 | async-start | bytes 15728640 | tf_op jit(solution)/shard_map/reduce_scatter | solution.py:24
  1479.1 220.1 %all-gather.21.cloned.1.call-start = ((), (), s32[]{:S(2)}) async-start(), calls=%async_computation.20 | async-start | bytes 4718592 | tf_op jit(solution)/shard_map/all_gather | solution.py:22
  1595.3 89.6 %collective-permute-start.5 = (f32[3072,256]{1,0:T(8,128)}, f32[3072,256]{1,0:T(8,128)}, u32[]{:S(2)}, u32[]{:S(2)}) collective-permute-start(f32[3072,256]{1,0:T(8,128)} %reduce-scatter.19.cloned.1.call-done), channel_id=1, source_target_pairs={{0,0},{2,1},{4,2},{6,3},{1,4},{3,5},{5,6},{7,7}} | collective-permute-start | bytes 9437192 | tf_op jit(solution)/shard_map/ppermute | solution.py:25
  1688.5 185.9 %reduce-scatter.21.cloned.1.call-start = ((), (), s32[]{:S(2)}) async-start(), calls=%async_computation.21 | async-start | bytes 15728640 | tf_op jit(solution)/shard_map/reduce_scatter | solution.py:24
  1758.3 220.1 %all-gather.23.cloned.1.call-start = ((), (), s32[]{:S(2)}) async-start(), calls=%async_computation.22 | async-start | bytes 4718592 | tf_op jit(solution)/shard_map/all_gather | solution.py:22
  1874.4 89.6 %collective-permute-start.6 = (f32[3072,256]{1,0:T(8,128)}, f32[3072,256]{1,0:T(8,128)}, u32[]{:S(2)}, u32[]{:S(2)}) collective-permute-start(f32[3072,256]{1,0:T(8,128)} %reduce-scatter.21.cloned.1.call-done), channel_id=1, source_target_pairs={{0,0},{2,1},{4,2},{6,3},{1,4},{3,5},{5,6},{7,7}} | collective-permute-start | bytes 9437192 | tf_op jit(solution)/shard_map/ppermute | solution.py:25
  1967.7 185.9 %reduce-scatter.23.cloned.1.call-start = ((), (), s32[]{:S(2)}) async-start(), calls=%async_computation.23 | async-start | bytes 15728640 | tf_op jit(solution)/shard_map/reduce_scatter | solution.py:24
  2153.6 89.6 %collective-permute-start.7 = (f32[3072,256]{1,0:T(8,128)}, f32[3072,256]{1,0:T(8,128)}, u32[]{:S(2)}, u32[]{:S(2)}) collective-permute-start(f32[3072,256]{1,0:T(8,128)} %reduce-scatter.23.cloned.1.call-done), channel_id=1, source_target_pairs={{0,0},{2,1},{4,2},{6,3},{1,4},{3,5},{5,6},{7,7}} | collective-permute-start | bytes 9437192 | tf_op jit(solution)/shard_map/ppermute | solution.py:25
Sparse Core Ops, SparseCore 0:
  12.0 12.3 all-gather.8
  83.6 115.9 reduce-scatter.8
  293.0 10.4 all-gather.10
  362.7 115.9 reduce-scatter.10
  572.1 10.4 all-gather.12
  641.9 115.9 reduce-scatter.12
  851.3 10.4 all-gather.14
  921.0 115.9 reduce-scatter.14
  1130.4 10.4 all-gather.16
  1200.1 115.9 reduce-scatter.16
  1409.5 10.4 all-gather.18
  1479.3 115.9 reduce-scatter.18
  1688.7 10.4 all-gather.20
  1758.4 115.9 reduce-scatter.20
  1967.8 10.4 all-gather.22
  2037.5 115.9 reduce-scatter.22
where the time goes:
time: 2280 us; the launch traced here: 2250 us
  waiting for transfers between devices  1010 us (44%)
  blocking collectives  517 us (23%)
  matrix products  472 us (21%)
  starting transfers between devices  202 us (9%)
  other arithmetic  34.6 us (2%)
    reduce_scatter x8, waiting for transfers between devices, local_sweeps(): folded = lax.psum_scatter(part_prod, 'col', scatter_dimension=0, tiled=True)  929 us
    psum x8, blocking collectives, local_sweeps(): lax.psum(jnp.sum(dang_col * x_cur, axis=0), ('col', 'row')) / vertex_count  517 us
    dot_general x8, matrix products, local_sweeps(): part_prod = jnp.dot(mat_tile, x_src, preferred_element_type=jnp.float32)  472 us
    ppermute x8, starting transfers between devices, local_sweeps(): aligned = lax.ppermute(folded, ('col', 'row'), perm=realign)  200 us
    all_gather x8, waiting for transfers between devices, local_sweeps(): lax.all_gather(x_cur.astype(jnp.bfloat16), 'row', axis=0, tiled=True)  84.8 us
  transfers between devices with their start and end apart: 24, of which 16 were waited for; matrix products, arithmetic and copies ran while one was open for 0% of the time, Pallas kernels for 0%

commit v1 on v0

v1 whole, which is shorter than its diff:
```python
import functools

import jax
import jax.numpy as jnp
from jax import lax
from jax.experimental import pallas as pl
from jax.experimental.pallas import tpu as pltpu
from jax.sharding import PartitionSpec as P

SWEEPS = 8
DAMPING = 0.85
MESH = pl.DeviceIdType.MESH

VERTS = 24576
VECS = 256
PIECE = 3072
ROWS = 12288
COLS = 6144
BR = 256
NB = PIECE // BR
CH = 32
RING = 4


def kernel(a_hbm, x_hbm, v_hbm, d_hbm, out_hbm,
           abuf, xbf, ybuf, ra, rgy, rdy, rfx, rfy, vbuf, dbuf, sbuf, s0buf, coef,
           a_sem, in_sem, ina_send, ina_recv,
           a_s, a_r, gy_s, gy_r, dy_s, dy_r, fx_s, fx_r, fy_s, fy_r,
           x_s, x_r, s_s, s_r, s0_s, s0_r, o_l, o_s, o_r,
           cr_hh, cr_hw, cr_gy, cr_ww, cr_x):
    col = lax.axis_index('col')
    row = lax.axis_index('row')
    cx, cy = lax.rem(col, 2), lax.div(col, 2)
    home = row == cy
    xn = (cy * 2 + 1 - cx, row)
    yn = ((1 - cy) * 2 + cx, row)
    mate = (col, 1 - row)
    same = cx * COLS
    other = (1 - cx) * COLS

    barrier = pltpu.get_barrier_semaphore()
    for off in range(4):
        for r in range(2):
            if off == 0 and r == 1:
                continue
            dev = (lax.rem(col + off, 4), row if r == 0 and off else 1 - row)
            pl.semaphore_signal(barrier, inc=1, device_id=dev, device_id_type=MESH)

    def blk(n):
        return pl.ds(pl.multiple_of(n * BR, BR), BR)

    def rows_at(base, t, b):
        return pl.ds(pl.multiple_of(base + t * PIECE + b * BR, BR), BR)

    def remote(src, dst, send, recv, dev):
        return pltpu.make_async_remote_copy(
            src_ref=src, dst_ref=dst, send_sem=send, recv_sem=recv, device_id=dev, device_id_type=MESH)

    def c_a(b):
        return remote(ybuf.at[rows_at(other, 0, b)], ra.at[blk(b)], a_s.at[b], a_r.at[b], xn)

    def c_gy(b):
        return remote(ybuf.at[rows_at(other, 1, b)], rgy.at[blk(b)], gy_s.at[b], gy_r.at[b], yn)

    def c_dy(b):
        return remote(ybuf.at[rows_at(same, 1, b)], rdy.at[blk(b)], dy_s.at[b], dy_r.at[b], yn)

    def c_fx(b):
        return remote(ybuf.at[rows_at(other, 1, b)], rfx.at[blk(b)], fx_s.at[b], fx_r.at[b], xn)

    def c_fy(b):
        return remote(ybuf.at[rows_at(same, 0, b)], rfy.at[blk(b)], fy_s.at[b], fy_r.at[b], yn)

    def c_x(n):
        return remote(xbf.at[blk(n)], xbf.at[blk(n)], x_s.at[n], x_r.at[n], mate)

    def block_of(n):
        m = lax.rem(n, 2 * NB)
        first = n < 2 * NB
        t = jnp.where(first, lax.rem(m, 2), 1 - lax.div(m, NB))
        b = jnp.where(first, lax.div(m, 2), lax.rem(m, NB))
        return jnp.where(first, other, same) + t * PIECE + b * BR

    def a_copy(n):
        slot = lax.rem(n, RING)
        start = pl.multiple_of(block_of(n), BR)
        return pltpu.make_async_copy(a_hbm.at[pl.ds(start, BR)], abuf.at[slot], a_sem.at[slot])

    x_in = pltpu.make_async_copy(x_hbm, ybuf.at[pl.ds(0, PIECE)], in_sem.at[0])
    x_in.start()
    piece = pl.ds(pl.multiple_of(row * PIECE, PIECE), PIECE)
    d_in = pltpu.make_async_copy(d_hbm, dbuf.at[piece], in_sem.at[1])
    d_in.start()
    for n in range(RING):
        a_copy(jnp.int32(n)).start()
    v_in = pltpu.make_async_copy(v_hbm, vbuf.at[piece], in_sem.at[2])

    @pl.when(home)
    def _():
        v_in.start()

    v_out = remote(v_hbm, vbuf.at[piece], ina_send.at[0], ina_recv.at[0], mate)
    d_out = remote(d_hbm, dbuf.at[piece], ina_send.at[1], ina_recv.at[1], mate)

    x_in.wait()
    d_in.wait()

    def convert(c, acc):
        x = ybuf[pl.ds(pl.multiple_of(c * CH, CH), CH), :]
        at = pl.ds(pl.multiple_of(row * PIECE + c * CH, CH), CH)
        d = dbuf[at, :]
        xbf[at, :] = x.astype(jnp.bfloat16)
        w = x * jnp.concatenate([d, d], axis=1)
        return acc + jnp.sum(w.reshape(CH // 8, 8, VECS), axis=0)

    s_own = lax.fori_loop(0, PIECE // CH, convert, jnp.zeros((8, VECS), jnp.float32))
    s0buf[row] = s_own
    pl.semaphore_wait(barrier, 7)

    s0_out = remote(s0buf.at[row], s0buf.at[row], s0_s, s0_r, mate)

    def x0_copy(r):
        at = pl.ds(pl.multiple_of(r * PIECE, PIECE), PIECE)
        return remote(xbf.at[at], xbf.at[at], ina_send.at[2], ina_recv.at[2], mate)

    x0_copy(row).start()

    @pl.when(jnp.logical_not(home))
    def _():
        v_out.start()
        d_out.start()
        s0_out.start()

    x0_copy(row).wait_send()
    x0_copy(1 - row).wait_recv()

    def s_copy(par, off):
        dst_col = lax.rem(col + off, 4)
        return remote(sbuf.at[par, col], sbuf.at[par, col], s_s.at[par, off], s_r.at[par, col],
                      (dst_col, lax.div(dst_col, 2)))

    def s_wait(par, off):
        src_col = lax.rem(col + off, 4)
        return remote(sbuf.at[par, src_col], sbuf.at[par, src_col], s_s.at[par, off], s_r.at[par, src_col],
                      (src_col, lax.div(src_col, 2)))

    def s_publish(par, value):
        sbuf[par, col] = value
        for off in range(1, 4):
            s_copy(par, off).start()

    def sweep(k, carry):
        last = k == SWEEPS - 1

        def multiply(n):
            slot = lax.rem(n, RING)
            a_copy(n).wait()
            start = pl.multiple_of(block_of(n), BR)
            ybuf[pl.ds(start, BR), :] = jnp.dot(abuf[slot], xbf[...], preferred_element_type=jnp.float32)
            after = n + RING

            @pl.when(jnp.logical_not(jnp.logical_and(last, after >= 4 * NB)))
            def _():
                a_copy(lax.rem(after, 4 * NB)).start()

        @pl.when(k > 0)
        def _():
            @pl.when(home)
            def _():
                pl.semaphore_wait(cr_hh, 1)

            @pl.when(jnp.logical_not(home))
            def _():
                pl.semaphore_wait(cr_ww, 1)
                pl.semaphore_wait(cr_gy, 1)

        def part_one(n, c):
            multiply(n)
            b = lax.div(n, 2)

            @pl.when(lax.rem(n, 2) == 0)
            def _():
                c_a(b).start()

            @pl.when(jnp.logical_and(lax.rem(n, 2) == 1, jnp.logical_not(home)))
            def _():
                c_gy(b).start()
            return c

        lax.fori_loop(0, 2 * NB, part_one, 0)

        @pl.when(jnp.logical_and(k > 0, jnp.logical_not(home)))
        def _():
            pl.semaphore_wait(cr_hw, 1)

        def part_two(n, c):
            multiply(n)

            @pl.when(jnp.logical_and(n < 3 * NB, jnp.logical_not(home)))
            def _():
                c_dy(n - 2 * NB).start()
            return c

        lax.fori_loop(2 * NB, 4 * NB, part_two, 0)

        def add_into(base, t, b, src):
            def step(c, z):
                at = pl.ds(pl.multiple_of(base + t * PIECE + b * BR + c * CH, CH), CH)
                ybuf[at, :] = ybuf[at, :] + src[pl.ds(pl.multiple_of(b * BR + c * CH, CH), CH), :]
                return z
            lax.fori_loop(0, BR // CH, step, 0)

        @pl.when(jnp.logical_not(home))
        def _away():
            @pl.when(jnp.logical_not(last))
            def _():
                pl.semaphore_signal(cr_x, inc=1, device_id=mate, device_id_type=MESH)

            def forward(b, c):
                c_a(b).wait()
                add_into(same, 0, b, ra)
                c_fy(b).start()
                return c
            lax.fori_loop(0, NB, forward, 0)

            @pl.when(jnp.logical_not(last))
            def _():
                pl.semaphore_signal(cr_ww, inc=1, device_id=xn, device_id_type=MESH)

            def drain(b, c):
                c_gy(b).wait_send()
                c_dy(b).wait_send()
                c_fy(b).wait_send()
                return c
            lax.fori_loop(0, NB, drain, 0)

            @pl.when(k == 0)
            def _():
                v_out.wait_send()
                d_out.wait_send()
                s0_out.wait_send()

            @pl.when(jnp.logical_not(last))
            def _():
                def take(n, c):
                    c_x(n).wait_recv()
                    return c
                lax.fori_loop(0, 2 * NB, take, 0)

        @pl.when(home)
        def _home():
            par = lax.rem(k, 2)

            @pl.when(k == 0)
            def _():
                v_in.wait()
                far = pl.ds(pl.multiple_of((1 - row) * PIECE, PIECE), PIECE)
                remote(v_hbm, vbuf.at[far], ina_send.at[0], ina_recv.at[0], mate).wait_recv()
                remote(d_hbm, dbuf.at[far], ina_send.at[1], ina_recv.at[1], mate).wait_recv()
                remote(s0buf.at[1 - row], s0buf.at[1 - row], s0_s, s0_r, mate).wait_recv()
                s_publish(0, s0buf[0] + s0buf[1])

            def forward(b, c):
                c_gy(b).wait_recv()
                add_into(other, 1, b, rgy)
                c_fx(b).start()
                return c
            lax.fori_loop(0, NB, forward, 0)

            @pl.when(jnp.logical_not(last))
            def _():
                pl.semaphore_signal(cr_gy, inc=1, device_id=yn, device_id_type=MESH)
                pl.semaphore_wait(cr_x, 1)

            for off in range(1, 4):
                s_wait(par, off).wait_recv()
                s_copy(par, off).wait_send()
            total = (sbuf[par, 0] + sbuf[par, 1]) + (sbuf[par, 2] + sbuf[par, 3])
            mass = jnp.sum(total, axis=0, keepdims=True) / VERTS
            coef[...] = jnp.broadcast_to(DAMPING * mass + (1.0 - DAMPING), (8, VECS))

            def update(t, b, one, two, acc):
                def step(c, acc):
                    at = pl.ds(pl.multiple_of(same + t * PIECE + b * BR + c * CH, CH), CH)
                    mine = pl.ds(pl.multiple_of(t * PIECE + b * BR + c * CH, CH), CH)
                    there = pl.ds(pl.multiple_of(b * BR + c * CH, CH), CH)
                    y = (ybuf[at, :] + one[there, :]) + two[there, :]
                    cf = jnp.concatenate([coef[...]] * (CH // 8), axis=0)
                    x = DAMPING * y + cf * vbuf[mine, :]
                    xbf[mine, :] = x.astype(jnp.bfloat16)
                    ybuf[at, :] = x
                    d = dbuf[mine, :]
                    w = x * jnp.concatenate([d, d], axis=1)
                    return acc + jnp.sum(w.reshape(CH // 8, 8, VECS), axis=0)
                return lax.fori_loop(0, BR // CH, step, acc)

            def finish_t(t, b):
                @pl.when(jnp.logical_not(last))
                def _():
                    c_x(t * NB + b).start()

                @pl.when(jnp.logical_and(last, row == t))
                def _():
                    pltpu.make_async_copy(ybuf.at[rows_at(same, t, b)], out_hbm.at[blk(b)], o_l.at[b]).start()

                @pl.when(jnp.logical_and(last, row != t))
                def _():
                    remote(ybuf.at[rows_at(same, t, b)], out_hbm.at[blk(b)], o_s.at[b], o_r.at[b], mate).start()

            def finish(b, acc):
                c_a(b).wait_recv()
                c_fy(b).wait_recv()
                acc = update(0, b, ra, rfy, acc)
                finish_t(0, b)
                c_dy(b).wait_recv()
                c_fx(b).wait_recv()
                acc = update(1, b, rdy, rfx, acc)
                finish_t(1, b)
                return acc

            s_new = lax.fori_loop(0, NB, finish, jnp.zeros((8, VECS), jnp.float32))

            @pl.when(jnp.logical_not(last))
            def _():
                pl.semaphore_signal(cr_hh, inc=1, device_id=xn, device_id_type=MESH)
                pl.semaphore_signal(cr_hw, inc=1, device_id=yn, device_id_type=MESH)
                s_publish(1 - par, s_new)

            def drain(b, c):
                c_a(b).wait_send()
                c_fx(b).wait_send()

                @pl.when(jnp.logical_not(last))
                def _():
                    c_x(b).wait_send()
                    c_x(NB + b).wait_send()
                return c
            lax.fori_loop(0, NB, drain, 0)

        return carry

    lax.fori_loop(0, SWEEPS, sweep, 0)

    def close(b, c):
        @pl.when(home)
        def _():
            pltpu.make_async_copy(ybuf.at[rows_at(same, row, b)], out_hbm.at[blk(b)], o_l.at[b]).wait()
            remote(ybuf.at[rows_at(same, 1 - row, b)], out_hbm.at[blk(b)], o_s.at[b], o_r.at[b], mate).wait_send()

        @pl.when(jnp.logical_not(home))
        def _():
            remote(ybuf.at[rows_at(same, 1 - row, b)], out_hbm.at[blk(b)], o_s.at[b], o_r.at[b], mate).wait_recv()
        return c

    lax.fori_loop(0, NB, close, 0)


def solution(mesh):
    dma = pltpu.SemaphoreType.DMA
    reg = pltpu.SemaphoreType.REGULAR

    def local_sweeps(mat_tile, x_piece, tele_piece, dang_piece):
        dang = jnp.broadcast_to(dang_piece.astype(jnp.float32)[:, None], (PIECE, 128))
        part = pltpu.VMEM((PIECE, VECS), jnp.float32)
        return pl.pallas_call(
            kernel,
            name="sweeps",
            out_shape=jax.ShapeDtypeStruct((PIECE, VECS), jnp.float32),
            in_specs=[pl.BlockSpec(memory_space=pl.ANY)] * 4,
            out_specs=pl.BlockSpec(memory_space=pl.ANY),
            scratch_shapes=[
                pltpu.VMEM((RING, BR, COLS), jnp.bfloat16),
                pltpu.VMEM((COLS, VECS), jnp.bfloat16),
                pltpu.VMEM((ROWS, VECS), jnp.float32),
                part, part, part, part, part,
                pltpu.VMEM((COLS, VECS), jnp.float32),
                pltpu.VMEM((COLS, 128), jnp.float32),
                pltpu.VMEM((2, 4, 8, VECS), jnp.float32),
                pltpu.VMEM((2, 8, VECS), jnp.float32),
                pltpu.VMEM((8, VECS), jnp.float32),
                dma((RING,)), dma((3,)), dma((3,)), dma((3,)),
                dma((NB,)), dma((NB,)), dma((NB,)), dma((NB,)), dma((NB,)), dma((NB,)),
                dma((NB,)), dma((NB,)), dma((NB,)), dma((NB,)),
                dma((2 * NB,)), dma((2 * NB,)), dma((2, 4)), dma((2, 4)), dma, dma,
                dma((NB,)), dma((NB,)), dma((NB,)),
                reg, reg, reg, reg, reg,
            ],
            compiler_params=pltpu.CompilerParams(
                collective_id=0, has_side_effects=True, vmem_limit_bytes=67_000_000),
            cost_estimate=pl.CostEstimate(
                flops=2 * ROWS * COLS * VECS * SWEEPS, bytes_accessed=2 * ROWS * COLS * SWEEPS, transcendentals=0),
        )(mat_tile, x_piece, tele_piece, dang)

    vec_spec = P(('col', 'row'), None)
    return jax.shard_map(local_sweeps, mesh=mesh,
                         in_specs=(P('row', 'col'), vec_spec, vec_spec, P(('col', 'row'))),
                         out_specs=vec_spec, check_vma=False)
```

time: 2280 us -> 872 us (0.38); the launches traced: 2250 us -> 872 us
  waiting for transfers between devices: 1010 us -> 0 us
  Pallas kernels: 0 us -> 866 us
  blocking collectives: 517 us -> 0 us
  matrix products: 472 us -> 0 us
  starting transfers between devices: 202 us -> 0 us
  other arithmetic: 34.6 us -> 0.71 us
    reduce_scatter x8 -> x0, waiting for transfers between devices: 929 us -> none  [local_sweeps(): folded = lax.psum_scatter(part_prod, 'col', scatter_dimension=0, tiled=True)]
    pallas_call x0 -> x1, Pallas kernels: none -> 866 us  [local_sweeps(): pl.pallas_call(kernel, name='sweeps', out_shape=jax.ShapeDtypeStruct((PIE...]
    psum x8 -> x0, blocking collectives: 517 us -> none  [local_sweeps(): lax.psum(jnp.sum(dang_col * x_cur, axis=0), ('col', 'row')) / vertex_count]
    dot_general x8 -> x0, matrix products: 472 us -> none  [local_sweeps(): part_prod = jnp.dot(mat_tile, x_src, preferred_element_type=jnp.float32)]
    ppermute x8 -> x0, starting transfers between devices: 200 us -> none  [local_sweeps(): aligned = lax.ppermute(folded, ('col', 'row'), perm=realign)]
    all_gather x8 -> x0, waiting for transfers between devices: 84.8 us -> none  [local_sweeps(): lax.all_gather(x_cur.astype(jnp.bfloat16), 'row', axis=0, tiled=True)]
    convert_element_type x8 -> x1, other arithmetic: 27 us -> 0.71 us  [local_sweeps(): dang_piece.astype(jnp.float32)[:, None]]
  transfers between devices with their start and end apart: 24 -> 0, of which waited for: 16 -> 0; matrix products, arithmetic and copies ran while one was open for 0% -> 0% of each run, Pallas kernels for 0% -> 0%
where the time goes in v1:
time: 872 us
  Pallas kernels  866 us (99%)
    pallas_call x1, Pallas kernels, local_sweeps(): pl.pallas_call(kernel, name='sweeps', out_shape=jax.ShapeDtypeStruct((PIE...  866 us

profile of v1, /device:TPU:0, one launch (start us, length us, event | category | flops | bytes accessed | tf_op | source)
XLA Modules:
  0.0 871.7 jit_solution(10782498417291213137)
XLA Ops:
  0.0 0.7 convert_element_type.3
  0.7 1.6 broadcast_in_dim.2.d_hbm
  2.3 865.6 %sweeps.1 = f32[3072,256]{1,0:T(8,128)} custom-call(bf16[12288,6144]{1,0:T(8,128)(2,1)} %a_hbm.1, f32[3072,256]{1,0:T(8,128)} %x_hbm.1, f32[3072,256]{1,0:T(8,128)} %v_hbm.1, f32[3072,128]{1,0:T(8,128)} %broadcast_in_dim.2.d_hbm), custom_call_target="tpu_custom_call" | custom-call | flops 309237645312 | bytes 1207959552 | tf_op jit(solution)/shard_map/sweeps/pallas_call | solution.py:365
  867.9 3.8 copy.6

commit v2 on v0

v2 whole, which is shorter than its diff:
```python
import jax
import jax.numpy as jnp
from jax import lax
from jax.experimental import pallas as pl
from jax.experimental.pallas import tpu as pltpu
from jax.sharding import PartitionSpec as P

SWEEPS = 8
DAMPING = 0.85
MESH = pl.DeviceIdType.MESH

VERTS = 24576
VECS = 256
HALF = 128
PIECE = 3072
ROWS = 12288
COLS = 6144
BR = 256
NB = PIECE // BR
G = 4
E = NB - G
CH = 32
RING = 4
X0C = 6
X0R = PIECE // X0C


def kernel(a_hbm, x_hbm, v_hbm, d_hbm, out_hbm,
           abuf, xbf, ybuf, ra, rgy, rdy, rfx, rfy, vbuf, dbuf, dint, sbuf, s0buf, coef, sacc,
           a_sem, xin_sem, in_sem, ina_send, ina_recv, x0_s, x0_r,
           a_s, a_r, gy_s, gy_r, dy_s, dy_r, fx_s, fx_r, fy_s, fy_r,
           x_s, x_r, s_s, s_r, s0_s, s0_r, o_l, o_s, o_r,
           cr_hh1, cr_hh2, cr_hw, cr_gy, cr_ww, cr_x):
    col = lax.axis_index('col')
    row = lax.axis_index('row')
    cx, cy = lax.rem(col, 2), lax.div(col, 2)
    home = row == cy
    away = jnp.logical_not(home)
    xn = (cy * 2 + 1 - cx, row)
    yn = ((1 - cy) * 2 + cx, row)
    mate = (col, 1 - row)
    same = cx * COLS
    other = (1 - cx) * COLS

    barrier = pltpu.get_barrier_semaphore()
    for off in range(4):
        for r in range(2):
            if off == 0 and r == 1:
                continue
            dev = (lax.rem(col + off, 4), row if r == 0 and off else 1 - row)
            pl.semaphore_signal(barrier, inc=1, device_id=dev, device_id_type=MESH)

    def signal(sem, dev):
        pl.semaphore_signal(sem, inc=1, device_id=dev, device_id_type=MESH)

    def rows_of(start, size):
        return pl.ds(pl.multiple_of(start, size), size)

    def blk(n):
        return rows_of(n * BR, BR)

    def cols(h):
        return pl.ds(0, VECS) if h is None else pl.ds(h * HALF, HALF)

    def slot_of(b, h, first):
        return b if h != 1 else NB + b - (0 if first else E)

    def remote(src, dst, send, recv, dev):
        return pltpu.make_async_remote_copy(
            src_ref=src, dst_ref=dst, send_sem=send, recv_sem=recv, device_id=dev, device_id_type=MESH)

    def flow(base, t, b, h, dst, send, recv, dev, first):
        i = slot_of(b, h, first)
        return remote(ybuf.at[rows_of(base + t * PIECE + b * BR, BR), cols(h)], dst.at[blk(b), cols(h)],
                      send.at[i], recv.at[i], dev)

    def c_a(b, h=None):
        return flow(other, 0, b, h, ra, a_s, a_r, xn, True)

    def c_gy(b, h=None):
        return flow(other, 1, b, h, rgy, gy_s, gy_r, yn, True)

    def c_dy(b):
        return flow(same, 1, b, None, rdy, dy_s, dy_r, yn, True)

    def c_fx(b, h=None):
        return flow(other, 1, b, h, rfx, fx_s, fx_r, xn, False)

    def c_fy(b, h=None):
        return flow(same, 0, b, h, rfy, fy_s, fy_r, yn, False)

    def c_x(t, b, h=None):
        at = rows_of(t * PIECE + b * BR, BR)
        i = t * (NB + G) + slot_of(b, h, False)
        return remote(xbf.at[at, cols(h)], xbf.at[at, cols(h)], x_s.at[i], x_r.at[i], mate)

    tf = jnp.where(home, 0, 1)

    def block_of(n):
        lead = n < 2 * G
        m = jnp.where(lead, n, n - 2 * G)
        t0 = jnp.where(lead, lax.div(m, G), lax.rem(m, 2))
        b0 = jnp.where(lead, lax.rem(m, G), G + lax.div(m, 2))
        t0 = jnp.where(t0 == 0, tf, 1 - tf)
        m = n - 2 * NB
        first = n < 2 * NB
        t = jnp.where(first, t0, 1 - lax.div(m, NB))
        b = jnp.where(first, b0, lax.rem(m, NB))
        return jnp.where(first, other, same) + t * PIECE + b * BR

    def a_copy(n):
        slot = lax.rem(n, RING)
        return pltpu.make_async_copy(a_hbm.at[rows_of(block_of(n), BR)], abuf.at[slot], a_sem.at[slot])

    def loop(lo, hi, body):
        def step(i, c):
            body(i)
            return c
        lax.fori_loop(lo, hi, step, 0)

    mine = row * PIECE
    far = (1 - row) * PIECE
    piece = rows_of(mine, PIECE)
    far_piece = rows_of(far, PIECE)

    def x_in(c):
        return pltpu.make_async_copy(x_hbm.at[rows_of(c * X0R, X0R)], vbuf.at[rows_of(mine + c * X0R, X0R)], xin_sem.at[c])

    def x0_copy(base, c):
        at = rows_of(base + c * X0R, X0R)
        return remote(xbf.at[at], xbf.at[at], x0_s.at[c], x0_r.at[c], mate)

    for c in range(X0C):
        x_in(c).start()
    d_in = pltpu.make_async_copy(d_hbm, dint.at[row], in_sem.at[0])
    v_in = pltpu.make_async_copy(v_hbm, vbuf.at[piece], in_sem.at[1])
    v_out = remote(v_hbm, vbuf.at[piece], ina_send.at[0], ina_recv.at[0], mate)
    d_out = remote(d_hbm, dint.at[row], ina_send.at[1], ina_recv.at[1], mate)
    s0_out = remote(s0buf.at[row], s0buf.at[row], s0_s, s0_r, mate)

    for c in range(X0C):
        x_in(c).wait()

        def convert(i, c=c):
            at = rows_of(mine + c * X0R + i * CH, CH)
            xbf[at, :] = vbuf[at, :].astype(jnp.bfloat16)
        loop(0, X0R // CH, convert)
        if c == 0:
            pl.semaphore_wait(barrier, 7)
        x0_copy(mine, c).start()
        if c < RING:
            a_copy(jnp.int32(c)).start()
    d_in.start()

    @pl.when(away)
    def _():
        d_out.start()
        v_out.start()

    for c in range(X0C):
        x0_copy(far, c).wait_recv()

    def s_copy(par, off):
        dst_col = lax.rem(col + off, 4)
        return remote(sbuf.at[par, col], sbuf.at[par, col], s_s.at[par, off], s_r.at[par, col],
                      (dst_col, lax.div(dst_col, 2)))

    def s_wait(par, off):
        src_col = lax.rem(col + off, 4)
        return remote(sbuf.at[par, src_col], sbuf.at[par, src_col], s_s.at[par, off], s_r.at[par, src_col],
                      (src_col, lax.div(src_col, 2)))

    def s_publish(par, value):
        sbuf[par, col] = value
        for off in range(1, 4):
            s_copy(par, off).start()

    def spread(r):
        def group(g):
            flags = dint[r, pl.ds(g, 1), :].astype(jnp.float32)
            dbuf[rows_of(r * PIECE + g * 128, 128), :] = jnp.broadcast_to(flags, (128, 128)).T
        loop(0, PIECE // 128, group)

    def first_mass():
        d_in.wait()
        spread(row)

        def add(c, acc):
            at = rows_of(mine + c * CH, CH)
            d = dbuf[at, :]
            w = vbuf[at, :] * jnp.concatenate([d, d], axis=1)
            return acc + jnp.sum(w.reshape(CH // 8, 8, VECS), axis=0)
        s0buf[row] = lax.fori_loop(0, PIECE // CH, add, jnp.zeros((8, VECS), jnp.float32))

    def update(t, b, h, one, two, acc):
        def step(c, acc):
            at = rows_of(same + t * PIECE + b * BR + c * CH, CH)
            own = rows_of(t * PIECE + b * BR + c * CH, CH)
            there = rows_of(b * BR + c * CH, CH)
            y = (ybuf[at, cols(h)] + one[there, cols(h)]) + two[there, cols(h)]
            cf = jnp.concatenate([coef[:, cols(h)]] * (CH // 8), axis=0)
            x = DAMPING * y + cf * vbuf[own, cols(h)]
            xbf[own, cols(h)] = x.astype(jnp.bfloat16)
            ybuf[at, cols(h)] = x
            d = dbuf[own, :]
            if h is None:
                d = jnp.concatenate([d, d], axis=1)
            return acc + jnp.sum((x * d).reshape(CH // 8, 8, d.shape[1]), axis=0)
        return lax.fori_loop(0, BR // CH, step, acc)

    def o_local(t, b, h):
        i = slot_of(b, h, False)
        return pltpu.make_async_copy(
            ybuf.at[rows_of(same + t * PIECE + b * BR, BR), cols(h)], out_hbm.at[blk(b), cols(h)], o_l.at[i])

    def o_remote(t, b, h):
        i = slot_of(b, h, False)
        return remote(ybuf.at[rows_of(same + t * PIECE + b * BR, BR), cols(h)], out_hbm.at[blk(b), cols(h)],
                      o_s.at[i], o_r.at[i], mate)

    def emit(t, b, h, last):
        @pl.when(jnp.logical_not(last))
        def _():
            c_x(t, b, h).start()

        @pl.when(jnp.logical_and(last, row == t))
        def _():
            o_local(t, b, h).start()

        @pl.when(jnp.logical_and(last, row != t))
        def _():
            o_remote(t, b, h).start()

    def finish(b, h, last, acc):
        acc = update(0, b, h, ra, rfy, acc)
        emit(0, b, h, last)
        acc = update(1, b, h, rdy, rfx, acc)
        emit(1, b, h, last)
        return acc

    def finish_half(h, last):
        def one(b, acc):
            if h == 0:
                c_a(b).wait()
                c_dy(b).wait_recv()
            c_fy(b, h).wait_recv()
            c_fx(b, h).wait_recv()
            return finish(b, h, last, acc)
        part = lax.fori_loop(E, NB, one, jnp.zeros((8, HALF), jnp.float32))
        sacc[:, cols(h)] = sacc[:, cols(h)] + part

    def drain_forward():
        @pl.when(home)
        def _():
            loop(0, E, lambda b: c_fx(b).wait_send())
            for h in range(2):
                loop(E, NB, lambda b: c_fx(b, h).wait_send())

        @pl.when(away)
        def _():
            loop(0, E, lambda b: c_fy(b).wait_send())
            for h in range(2):
                loop(E, NB, lambda b: c_fy(b, h).wait_send())

    def sweep(k, carry):
        last = k == SWEEPS - 1
        par = lax.rem(k, 2)

        def multiply(n, h):
            start = block_of(n)
            ybuf[rows_of(start, BR), cols(h)] = jnp.dot(
                abuf[lax.rem(n, RING)], xbf[:, cols(h)], preferred_element_type=jnp.float32)

        def fetch(n):
            @pl.when(jnp.logical_not(jnp.logical_and(last, n >= 4 * NB)))
            def _():
                a_copy(lax.rem(n, 4 * NB)).start()

        @pl.when(k > 0)
        def _():
            @pl.when(home)
            def _():
                pl.semaphore_wait(cr_hh1, 1)

            @pl.when(away)
            def _():
                pl.semaphore_wait(cr_gy, 1)

        def lead(h):
            def one(n):
                if h == 0:
                    a_copy(n).wait()
                multiply(n, h)
                if h == 1:
                    fetch(n + RING)

                @pl.when(home)
                def _():
                    c_a(n, h).start()

                @pl.when(away)
                def _():
                    c_gy(n, h).start()
            loop(0, G, one)

        lead(0)

        @pl.when(k > 0)
        def _():
            @pl.when(home)
            def _():
                finish_half(1, jnp.bool_(False))
                s_publish(par, sacc[...])
                signal(cr_hh2, xn)
                signal(cr_hw, yn)

            @pl.when(away)
            def _():
                for t in range(2):
                    loop(E, NB, lambda b: c_x(t, b, 1).wait_recv())

        lead(1)

        @pl.when(k > 0)
        def _():
            drain_forward()

            @pl.when(home)
            def _():
                pl.semaphore_wait(cr_hh2, 1)

            @pl.when(away)
            def _():
                pl.semaphore_wait(cr_ww, 1)
                pl.semaphore_wait(cr_hw, 1)

        def rest(n):
            a_copy(n).wait()
            multiply(n, None)
            fetch(n + RING)
            start = block_of(n)
            first = n < 2 * NB
            at = start - jnp.where(first, other, same)
            t, b = lax.div(at, PIECE), lax.div(lax.rem(at, PIECE), BR)

            @pl.when(jnp.logical_and(first, t == 0))
            def _():
                c_a(b).start()

            @pl.when(jnp.logical_and(jnp.logical_and(first, t == 1), away))
            def _():
                c_gy(b).start()

            @pl.when(jnp.logical_and(jnp.logical_and(jnp.logical_not(first), t == 1), away))
            def _():
                c_dy(b).start()

        loop(G, 4 * NB, rest)

        def add_into(base, t, b, src):
            def step(c):
                at = rows_of(base + t * PIECE + b * BR + c * CH, CH)
                ybuf[at, :] = ybuf[at, :] + src[rows_of(b * BR + c * CH, CH), :]
            loop(0, BR // CH, step)

        @pl.when(away)
        def _away():
            @pl.when(k == 0)
            def _():
                for c in range(X0C):
                    x0_copy(mine, c).wait_send()

            @pl.when(jnp.logical_not(last))
            def _():
                signal(cr_x, mate)

            @pl.when(k == 0)
            def _():
                first_mass()
                s0_out.start()

            def forward(b):
                c_a(b).wait()
                add_into(same, 0, b, ra)

            def forward_full(b):
                forward(b)
                c_fy(b).start()

            def forward_half(b):
                forward(b)
                c_fy(b, 0).start()
            loop(0, E, forward_full)
            loop(E, NB, forward_half)
            loop(E, NB, lambda b: c_fy(b, 1).start())

            @pl.when(jnp.logical_not(last))
            def _():
                signal(cr_ww, xn)

            for h in range(2):
                loop(0, G, lambda b: c_gy(b, h).wait_send())
            loop(G, NB, lambda b: c_gy(b).wait_send())
            loop(0, NB, lambda b: c_dy(b).wait_send())

            @pl.when(k == 0)
            def _():
                v_out.wait_send()
                d_out.wait_send()
                s0_out.wait_send()

            @pl.when(jnp.logical_not(last))
            def _():
                for t in range(2):
                    loop(0, E, lambda b: c_x(t, b).wait_recv())
                    loop(E, NB, lambda b: c_x(t, b, 0).wait_recv())

        @pl.when(home)
        def _home():
            def forward(b):
                add_into(other, 1, b, rgy)

            def forward_a(b):
                c_gy(b, 0).wait_recv()
                c_gy(b, 1).wait_recv()
                forward(b)
                c_fx(b).start()

            def forward_b(b):
                c_gy(b).wait_recv()
                forward(b)
                c_fx(b).start()

            def forward_c(b):
                c_gy(b).wait_recv()
                forward(b)
                c_fx(b, 0).start()
            loop(0, G, forward_a)
            loop(G, E, forward_b)
            loop(E, NB, forward_c)
            loop(E, NB, lambda b: c_fx(b, 1).start())

            @pl.when(jnp.logical_not(last))
            def _():
                signal(cr_gy, yn)

            @pl.when(k == 0)
            def _():
                first_mass()
                v_in.start()
                remote(d_hbm, dint.at[1 - row], ina_send.at[1], ina_recv.at[1], mate).wait_recv()
                spread(1 - row)
                remote(s0buf.at[1 - row], s0buf.at[1 - row], s0_s, s0_r, mate).wait_recv()
                s_publish(0, s0buf[0] + s0buf[1])
                for c in range(X0C):
                    x0_copy(mine, c).wait_send()
                remote(v_hbm, vbuf.at[far_piece], ina_send.at[0], ina_recv.at[0], mate).wait_recv()
                v_in.wait()

            @pl.when(k > 0)
            def _():
                for t in range(2):
                    loop(0, E, lambda b: c_x(t, b).wait_send())
                    for h in range(2):
                        loop(E, NB, lambda b: c_x(t, b, h).wait_send())

            for off in range(1, 4):
                s_wait(par, off).wait_recv()
                s_copy(par, off).wait_send()
            total = (sbuf[par, 0] + sbuf[par, 1]) + (sbuf[par, 2] + sbuf[par, 3])
            mass = jnp.sum(total, axis=0, keepdims=True) / VERTS
            coef[...] = jnp.broadcast_to(DAMPING * mass + (1.0 - DAMPING), (8, VECS))

            @pl.when(jnp.logical_not(last))
            def _():
                pl.semaphore_wait(cr_x, 1)

            def full(b, acc, halves):
                if halves:
                    c_a(b, 0).wait()
                    c_a(b, 1).wait()
                else:
                    c_a(b).wait()
                c_fy(b).wait_recv()
                acc = update(0, b, None, ra, rfy, acc)
                emit(0, b, None, last)
                c_dy(b).wait_recv()
                c_fx(b).wait_recv()
                acc = update(1, b, None, rdy, rfx, acc)
                emit(1, b, None, last)
                return acc

            acc = lax.fori_loop(0, G, lambda b, acc: full(b, acc, True), jnp.zeros((8, VECS), jnp.float32))
            acc = lax.fori_loop(G, E, lambda b, acc: full(b, acc, False), acc)
            sacc[...] = acc

            @pl.when(jnp.logical_not(last))
            def _():
                signal(cr_hh1, xn)
            finish_half(0, last)

        return carry

    lax.fori_loop(0, SWEEPS, sweep, 0)

    @pl.when(home)
    def _():
        finish_half(1, jnp.bool_(True))
    drain_forward()

    @pl.when(home)
    def _():
        def close(b, h):
            o_local(row, b, h).wait()
            o_remote(1 - row, b, h).wait_send()
        loop(0, E, lambda b: close(b, None))
        for h in range(2):
            loop(E, NB, lambda b: close(b, h))

    @pl.when(away)
    def _():
        loop(0, E, lambda b: o_remote(1 - row, b, None).wait_recv())
        for h in range(2):
            loop(E, NB, lambda b: o_remote(1 - row, b, h).wait_recv())


def solution(mesh):
    dma = pltpu.SemaphoreType.DMA
    reg = pltpu.SemaphoreType.REGULAR

    def local_sweeps(mat_tile, x_piece, tele_piece, dang_piece):
        part = pltpu.VMEM((PIECE, VECS), jnp.float32)
        return pl.pallas_call(
            kernel,
            name="sweeps",
            out_shape=jax.ShapeDtypeStruct((PIECE, VECS), jnp.float32),
            in_specs=[pl.BlockSpec(memory_space=pl.ANY)] * 4,
            out_specs=pl.BlockSpec(memory_space=pl.ANY),
            scratch_shapes=[
                pltpu.VMEM((RING, BR, COLS), jnp.bfloat16),
                pltpu.VMEM((COLS, VECS), jnp.bfloat16),
                pltpu.VMEM((ROWS, VECS), jnp.float32),
                part, part, part, part, part,
                pltpu.VMEM((COLS, VECS), jnp.float32),
                pltpu.VMEM((COLS, 128), jnp.float32),
                pltpu.VMEM((2, PIECE // 128, 128), jnp.int32),
                pltpu.VMEM((2, 4, 8, VECS), jnp.float32),
                pltpu.VMEM((2, 8, VECS), jnp.float32),
                pltpu.VMEM((8, VECS), jnp.float32),
                pltpu.VMEM((8, VECS), jnp.float32),
                dma((RING,)), dma((X0C,)), dma((2,)), dma((2,)), dma((2,)), dma((X0C,)), dma((X0C,)),
                dma((NB + G,)), dma((NB + G,)), dma((NB + G,)), dma((NB + G,)), dma((NB,)), dma((NB,)),
                dma((NB + G,)), dma((NB + G,)), dma((NB + G,)), dma((NB + G,)),
                dma((2 * (NB + G),)), dma((2 * (NB + G),)), dma((2, 4)), dma((2, 4)), dma, dma,
                dma((NB + G,)), dma((NB + G,)), dma((NB + G,)),
                reg, reg, reg, reg, reg, reg,
            ],
            compiler_params=pltpu.CompilerParams(
                collective_id=0, has_side_effects=True, vmem_limit_bytes=67_000_000),
            cost_estimate=pl.CostEstimate(
                flops=2 * ROWS * COLS * VECS * SWEEPS, bytes_accessed=2 * ROWS * COLS * SWEEPS, transcendentals=0),
        )(mat_tile, x_piece, tele_piece, dang_piece.reshape(PIECE // 128, 128))

    vec_spec = P(('col', 'row'), None)
    return jax.shard_map(local_sweeps, mesh=mesh,
                         in_specs=(P('row', 'col'), vec_spec, vec_spec, P(('col', 'row'))),
                         out_specs=vec_spec, check_vma=False)
```

time: 2280 us -> 844 us (0.37); the launches traced: 2250 us -> 844 us
  waiting for transfers between devices: 1010 us -> 0 us
  Pallas kernels: 0 us -> 840 us
  blocking collectives: 517 us -> 0 us
  matrix products: 472 us -> 0 us
  starting transfers between devices: 202 us -> 0 us
  other arithmetic: 34.6 us -> 0 us
    reduce_scatter x8 -> x0, waiting for transfers between devices: 929 us -> none  [local_sweeps(): folded = lax.psum_scatter(part_prod, 'col', scatter_dimension=0, tiled=True)]
    pallas_call x0 -> x1, Pallas kernels: none -> 840 us  [local_sweeps(): pl.pallas_call(kernel, name='sweeps', out_shape=jax.ShapeDtypeStruct((PIE...]
    psum x8 -> x0, blocking collectives: 517 us -> none  [local_sweeps(): lax.psum(jnp.sum(dang_col * x_cur, axis=0), ('col', 'row')) / vertex_count]
    dot_general x8 -> x0, matrix products: 472 us -> none  [local_sweeps(): part_prod = jnp.dot(mat_tile, x_src, preferred_element_type=jnp.float32)]
    ppermute x8 -> x0, starting transfers between devices: 200 us -> none  [local_sweeps(): aligned = lax.ppermute(folded, ('col', 'row'), perm=realign)]
    all_gather x8 -> x0, waiting for transfers between devices: 84.8 us -> none  [local_sweeps(): lax.all_gather(x_cur.astype(jnp.bfloat16), 'row', axis=0, tiled=True)]
    convert_element_type x8 -> x0, other arithmetic: 27 us -> none  [the longest x7 26.3 us: local_sweeps(): x_cur.astype(jnp.bfloat16)]
  transfers between devices with their start and end apart: 24 -> 0, of which waited for: 16 -> 0; matrix products, arithmetic and copies ran while one was open for 0% -> 0% of each run, Pallas kernels for 0% -> 0%
where the time goes in v2:
time: 844 us
  Pallas kernels  840 us (100%)
    pallas_call x1, Pallas kernels, local_sweeps(): pl.pallas_call(kernel, name='sweeps', out_shape=jax.ShapeDtypeStruct((PIE...  840 us

profile of v2, /device:TPU:0, one launch (start us, length us, event | category | flops | bytes accessed | tf_op | source)
XLA Modules:
  0.0 844.2 jit_solution(13594309353194681745)
XLA Ops:
  0.0 840.5 %sweeps.1 = f32[3072,256]{1,0:T(8,128)} custom-call(bf16[12288,6144]{1,0:T(8,128)(2,1)} %a_hbm.1, f32[3072,256]{1,0:T(8,128)} %x_hbm.1, f32[3072,256]{1,0:T(8,128)} %v_hbm.1, s32[24,128]{1,0:T(8,128)} %bitcast.1), custom_call_target="tpu_custom_call" | custom-call | flops 309237645312 | bytes 1207959552 | tf_op jit(solution)/shard_map/sweeps/pallas_call | solution.py:533
  840.5 3.8 copy.6

commit v3 on v2

--- a/solution.py
+++ b/solution.py
@@ -94,14 +94,13 @@
         i = t * (NB + G) + slot_of(b, h, False)
         return remote(xbf.at[at, cols(h)], xbf.at[at, cols(h)], x_s.at[i], x_r.at[i], mate)
 
-    tf = jnp.where(home, 0, 1)
-
     def block_of(n):
-        lead = n < 2 * G
-        m = jnp.where(lead, n, n - 2 * G)
-        t0 = jnp.where(lead, lax.div(m, G), lax.rem(m, 2))
-        b0 = jnp.where(lead, lax.rem(m, G), G + lax.div(m, 2))
-        t0 = jnp.where(t0 == 0, tf, 1 - tf)
+        m = n - G
+        pair = m < 2 * E
+        t0 = jnp.where(pair, lax.rem(m, 2), 1)
+        b0 = jnp.where(pair, jnp.where(t0 == 0, G, 0) + lax.div(m, 2), m - E)
+        b0 = jnp.where(m < 0, n, b0)
+        t0 = jnp.where(jnp.logical_xor(home, jnp.logical_or(m < 0, t0 == 0)), 1, 0)
         m = n - 2 * NB
         first = n < 2 * NB
         t = jnp.where(first, t0, 1 - lax.div(m, NB))

time: 844 us -> 837 us (level)
  no operation moved by 1% of the time
where the time goes in v3:
time: 837 us
  Pallas kernels  833 us (100%)
    pallas_call x1, Pallas kernels, local_sweeps(): pl.pallas_call(kernel, name='sweeps', out_shape=jax.ShapeDtypeStruct((PIE...  833 us

profile of v3, /device:TPU:0, one launch (start us, length us, event | category | flops | bytes accessed | tf_op | source)
XLA Modules:
  0.0 836.9 jit_solution(14320602363451687006)
XLA Ops:
  0.0 833.2 %sweeps.1 = f32[3072,256]{1,0:T(8,128)} custom-call(bf16[12288,6144]{1,0:T(8,128)(2,1)} %a_hbm.1, f32[3072,256]{1,0:T(8,128)} %x_hbm.1, f32[3072,256]{1,0:T(8,128)} %v_hbm.1, s32[24,128]{1,0:T(8,128)} %bitcast.1), custom_call_target="tpu_custom_call" | custom-call | flops 309237645312 | bytes 1207959552 | tf_op jit(solution)/shard_map/sweeps/pallas_call | solution.py:532
  833.2 3.8 copy.6

commit v4 on v3

--- a/solution.py
+++ b/solution.py
@@ -20,6 +20,13 @@
 G = 4
 E = NB - G
 CH = 32
+LEAD = (1, 2)
+TAIL = (2, 2)
+UA_HOME = 4
+UA_AWAY = 2
+UG = 2
+UD = 6
+UF = 4
 RING = 4
 X0C = 6
 X0R = PIECE // X0C
@@ -56,42 +63,44 @@
     def rows_of(start, size):
         return pl.ds(pl.multiple_of(start, size), size)
 
-    def blk(n):
-        return rows_of(n * BR, BR)
+    def blk(b, n):
+        return pl.ds(pl.multiple_of(b * BR, BR), n * BR)
 
     def cols(h):
         return pl.ds(0, VECS) if h is None else pl.ds(h * HALF, HALF)
 
-    def slot_of(b, h, first):
-        return b if h != 1 else NB + b - (0 if first else E)
+    def slot_of(b, h):
+        return b if h != 1 else NB + b
 
     def remote(src, dst, send, recv, dev):
         return pltpu.make_async_remote_copy(
             src_ref=src, dst_ref=dst, send_sem=send, recv_sem=recv, device_id=dev, device_id_type=MESH)
 
-    def flow(base, t, b, h, dst, send, recv, dev, first):
-        i = slot_of(b, h, first)
-        return remote(ybuf.at[rows_of(base + t * PIECE + b * BR, BR), cols(h)], dst.at[blk(b), cols(h)],
-                      send.at[i], recv.at[i], dev)
-
-    def c_a(b, h=None):
-        return flow(other, 0, b, h, ra, a_s, a_r, xn, True)
-
-    def c_gy(b, h=None):
-        return flow(other, 1, b, h, rgy, gy_s, gy_r, yn, True)
+    def y_rows(base, t, b, n):
+        return pl.ds(pl.multiple_of(base + t * PIECE + b * BR, BR), n * BR)
+
+    def flow(base, t, b, n, h, dst, send, recv, dev):
+        i = slot_of(b, h)
+        return remote(ybuf.at[y_rows(base, t, b, n), cols(h)], dst.at[blk(b, n), cols(h)], send.at[i], recv.at[i], dev)
+
+    def c_a(b, n, h=None):
+        return flow(other, 0, b, n, h, ra, a_s, a_r, xn)
+
+    def c_gy(b, n, h=None):
+        return flow(other, 1, b, n, h, rgy, gy_s, gy_r, yn)
 
     def c_dy(b):
-        return flow(same, 1, b, None, rdy, dy_s, dy_r, yn, True)
-
-    def c_fx(b, h=None):
-        return flow(other, 1, b, h, rfx, fx_s, fx_r, xn, False)
-
-    def c_fy(b, h=None):
-        return flow(same, 0, b, h, rfy, fy_s, fy_r, yn, False)
-
-    def c_x(t, b, h=None):
-        at = rows_of(t * PIECE + b * BR, BR)
-        i = t * (NB + G) + slot_of(b, h, False)
+        return flow(same, 1, b, UD, None, rdy, dy_s, dy_r, yn)
+
+    def c_fx(b, n, h=None):
+        return flow(other, 1, b, n, h, rfx, fx_s, fx_r, xn)
+
+    def c_fy(b, n, h=None):
+        return flow(same, 0, b, n, h, rfy, fy_s, fy_r, yn)
+
+    def c_x(t, b, n, h=None):
+        at = pl.ds(pl.multiple_of(t * PIECE + b * BR, BR), n * BR)
+        i = t * 2 * NB + slot_of(b, h)
         return remote(xbf.at[at, cols(h)], xbf.at[at, cols(h)], x_s.at[i], x_r.at[i], mate)
 
     def block_of(n):
@@ -117,6 +126,18 @@
             return c
         lax.fori_loop(lo, hi, step, 0)
 
+    def units(lo, hi, n, body):
+        loop(0, (hi - lo) // n, lambda u: body(lo + u * n))
+
+    def lead_units(h, body):
+        units(0, G, LEAD[h], lambda b: body(b, LEAD[h], h))
+
+    def tail_units(h, body):
+        units(E, NB, TAIL[h], lambda b: body(b, TAIL[h], h))
+
+    def forward_units(body):
+        units(0, E, UF, lambda b: body(b, UF, None))
+
     mine = row * PIECE
     far = (1 - row) * PIECE
     piece = rows_of(mine, PIECE)
@@ -191,7 +212,7 @@
             return acc + jnp.sum(w.reshape(CH // 8, 8, VECS), axis=0)
         s0buf[row] = lax.fori_loop(0, PIECE // CH, add, jnp.zeros((8, VECS), jnp.float32))
 
-    def update(t, b, h, one, two, acc):
+    def update(t, b, n, h, one, two, acc):
         def step(c, acc):
             at = rows_of(same + t * PIECE + b * BR + c * CH, CH)
             own = rows_of(t * PIECE + b * BR + c * CH, CH)
@@ -205,61 +226,56 @@
             if h is None:
                 d = jnp.concatenate([d, d], axis=1)
             return acc + jnp.sum((x * d).reshape(CH // 8, 8, d.shape[1]), axis=0)
-        return lax.fori_loop(0, BR // CH, step, acc)
-
-    def o_local(t, b, h):
-        i = slot_of(b, h, False)
+        return lax.fori_loop(0, n * BR // CH, step, acc)
+
+    def o_local(t, b, n, h):
         return pltpu.make_async_copy(
-            ybuf.at[rows_of(same + t * PIECE + b * BR, BR), cols(h)], out_hbm.at[blk(b), cols(h)], o_l.at[i])
-
-    def o_remote(t, b, h):
-        i = slot_of(b, h, False)
-        return remote(ybuf.at[rows_of(same + t * PIECE + b * BR, BR), cols(h)], out_hbm.at[blk(b), cols(h)],
-                      o_s.at[i], o_r.at[i], mate)
-
-    def emit(t, b, h, last):
+            ybuf.at[y_rows(same, t, b, n), cols(h)], out_hbm.at[blk(b, n), cols(h)], o_l.at[slot_of(b, h)])
+
+    def o_remote(t, b, n, h):
+        i = slot_of(b, h)
+        return remote(ybuf.at[y_rows(same, t, b, n), cols(h)], out_hbm.at[blk(b, n), cols(h)], o_s.at[i], o_r.at[i], mate)
+
+    def emit(t, b, n, h, last):
         @pl.when(jnp.logical_not(last))
         def _():
-            c_x(t, b, h).start()
+            c_x(t, b, n, h).start()
 
         @pl.when(jnp.logical_and(last, row == t))
         def _():
-            o_local(t, b, h).start()
+            o_local(t, b, n, h).start()
 
         @pl.when(jnp.logical_and(last, row != t))
         def _():
-            o_remote(t, b, h).start()
-
-    def finish(b, h, last, acc):
-        acc = update(0, b, h, ra, rfy, acc)
-        emit(0, b, h, last)
-        acc = update(1, b, h, rdy, rfx, acc)
-        emit(1, b, h, last)
+            o_remote(t, b, n, h).start()
+
+    def finish(b, n, h, last, acc):
+        c_fy(b, n, h).wait_recv()
+        acc = update(0, b, n, h, ra, rfy, acc)
+        emit(0, b, n, h, last)
+        c_fx(b, n, h).wait_recv()
+        acc = update(1, b, n, h, rdy, rfx, acc)
+        emit(1, b, n, h, last)
         return acc
 
     def finish_half(h, last):
-        def one(b, acc):
-            if h == 0:
-                c_a(b).wait()
-                c_dy(b).wait_recv()
-            c_fy(b, h).wait_recv()
-            c_fx(b, h).wait_recv()
-            return finish(b, h, last, acc)
-        part = lax.fori_loop(E, NB, one, jnp.zeros((8, HALF), jnp.float32))
+        n = TAIL[h]
+        part = lax.fori_loop(
+            0, G // n, lambda u, acc: finish(E + u * n, n, h, last, acc), jnp.zeros((8, HALF), jnp.float32))
         sacc[:, cols(h)] = sacc[:, cols(h)] + part
 
     def drain_forward():
         @pl.when(home)
         def _():
-            loop(0, E, lambda b: c_fx(b).wait_send())
-            for h in range(2):
-                loop(E, NB, lambda b: c_fx(b, h).wait_send())
+            forward_units(lambda b, n, h: c_fx(b, n, h).wait_send())
+            for half in range(2):
+                tail_units(half, lambda b, n, h: c_fx(b, n, h).wait_send())
 
         @pl.when(away)
         def _():
-            loop(0, E, lambda b: c_fy(b).wait_send())
-            for h in range(2):
-                loop(E, NB, lambda b: c_fy(b, h).wait_send())
+            forward_units(lambda b, n, h: c_fy(b, n, h).wait_send())
+            for half in range(2):
+                tail_units(half, lambda b, n, h: c_fy(b, n, h).wait_send())
 
     def sweep(k, carry):
         last = k == SWEEPS - 1
@@ -292,14 +308,17 @@
                 multiply(n, h)
                 if h == 1:
                     fetch(n + RING)
-
-                @pl.when(home)
+                size = LEAD[h]
+                whole = lax.rem(n, size) == size - 1
+                b = n - (size - 1)
+
+                @pl.when(jnp.logical_and(whole, home))
                 def _():
-                    c_a(n, h).start()
-
-                @pl.when(away)
+                    c_a(b, size, h).start()
+
+                @pl.when(jnp.logical_and(whole, away))
                 def _():
-                    c_gy(n, h).start()
+                    c_gy(b, size, h).start()
             loop(0, G, one)
 
         lead(0)
@@ -316,7 +335,7 @@
             @pl.when(away)
             def _():
                 for t in range(2):
-                    loop(E, NB, lambda b: c_x(t, b, 1).wait_recv())
+                    tail_units(1, lambda b, n, h: c_x(t, b, n, h).wait_recv())
 
         lead(1)
 
@@ -342,25 +361,27 @@
             at = start - jnp.where(first, other, same)
             t, b = lax.div(at, PIECE), lax.div(lax.rem(at, PIECE), BR)
 
-            @pl.when(jnp.logical_and(first, t == 0))
-            def _():
-                c_a(b).start()
-
-            @pl.when(jnp.logical_and(jnp.logical_and(first, t == 1), away))
-            def _():
-                c_gy(b).start()
-
-            @pl.when(jnp.logical_and(jnp.logical_and(jnp.logical_not(first), t == 1), away))
-            def _():
-                c_dy(b).start()
+            def send_when(cond, b0, size, start):
+                whole = lax.rem(b - b0, size) == size - 1
+
+                @pl.when(jnp.logical_and(cond, whole))
+                def _():
+                    start(b - (size - 1), size)
+
+            straight = jnp.logical_and(first, t == 0)
+            send_when(jnp.logical_and(straight, home), G, UA_HOME, lambda b, n: c_a(b, n).start())
+            send_when(jnp.logical_and(straight, away), 0, UA_AWAY, lambda b, n: c_a(b, n).start())
+            send_when(jnp.logical_and(jnp.logical_and(first, t == 1), away), G, UG, lambda b, n: c_gy(b, n).start())
+            send_when(jnp.logical_and(jnp.logical_and(jnp.logical_not(first), t == 1), away), 0, UD,
+                      lambda b, n: c_dy(b).start())
 
         loop(G, 4 * NB, rest)
 
-        def add_into(base, t, b, src):
+        def add_into(base, t, b, n, src):
             def step(c):
                 at = rows_of(base + t * PIECE + b * BR + c * CH, CH)
                 ybuf[at, :] = ybuf[at, :] + src[rows_of(b * BR + c * CH, CH), :]
-            loop(0, BR // CH, step)
+            loop(0, n * BR // CH, step)
 
         @pl.when(away)
         def _away():
@@ -378,29 +399,29 @@
                 first_mass()
                 s0_out.start()
 
-            def forward(b):
-                c_a(b).wait()
-                add_into(same, 0, b, ra)
-
-            def forward_full(b):
-                forward(b)
-                c_fy(b).start()
-
-            def forward_half(b):
-                forward(b)
-                c_fy(b, 0).start()
-            loop(0, E, forward_full)
-            loop(E, NB, forward_half)
-            loop(E, NB, lambda b: c_fy(b, 1).start())
+            def forward(b, n):
+                units(0, n, UA_AWAY, lambda i: c_a(b + i, UA_AWAY).wait())
+                add_into(same, 0, b, n, ra)
+
+            def forward_full(b, n, h):
+                forward(b, n)
+                c_fy(b, n).start()
+
+            def forward_half(b, n, h):
+                forward(b, n)
+                c_fy(b, n, h).start()
+            forward_units(forward_full)
+            tail_units(0, forward_half)
+            tail_units(1, lambda b, n, h: c_fy(b, n, h).start())
 
             @pl.when(jnp.logical_not(last))
             def _():
                 signal(cr_ww, xn)
 
-            for h in range(2):
-                loop(0, G, lambda b: c_gy(b, h).wait_send())
-            loop(G, NB, lambda b: c_gy(b).wait_send())
-            loop(0, NB, lambda b: c_dy(b).wait_send())
+            for half in range(2):
+                lead_units(half, lambda b, n, h: c_gy(b, n, h).wait_send())
+            units(G, NB, UG, lambda b: c_gy(b, UG).wait_send())
+            units(0, NB, UD, lambda b: c_dy(b).wait_send())
 
             @pl.when(k == 0)
             def _():
@@ -411,33 +432,31 @@
             @pl.when(jnp.logical_not(last))
             def _():
                 for t in range(2):
-                    loop(0, E, lambda b: c_x(t, b).wait_recv())
-                    loop(E, NB, lambda b: c_x(t, b, 0).wait_recv())
+                    forward_units(lambda b, n, h: c_x(t, b, n, h).wait_recv())
+                    tail_units(0, lambda b, n, h: c_x(t, b, n, h).wait_recv())
 
         @pl.when(home)
         def _home():
-            def forward(b):
-                add_into(other, 1, b, rgy)
-
-            def forward_a(b):
-                c_gy(b, 0).wait_recv()
-                c_gy(b, 1).wait_recv()
-                forward(b)
-                c_fx(b).start()
-
-            def forward_b(b):
-                c_gy(b).wait_recv()
-                forward(b)
-                c_fx(b).start()
-
-            def forward_c(b):
-                c_gy(b).wait_recv()
-                forward(b)
-                c_fx(b, 0).start()
-            loop(0, G, forward_a)
-            loop(G, E, forward_b)
-            loop(E, NB, forward_c)
-            loop(E, NB, lambda b: c_fx(b, 1).start())
+            for half in range(2):
+                lead_units(half, lambda b, n, h: c_gy(b, n, h).wait_recv())
+
+            def arrived(b, n):
+                @pl.when(b >= G)
+                def _():
+                    units(0, n, UG, lambda i: c_gy(b + i, UG).wait_recv())
+
+            def forward_full(b, n, h):
+                arrived(b, n)
+                add_into(other, 1, b, n, rgy)
+                c_fx(b, n).start()
+
+            def forward_half(b, n, h):
+                arrived(b, n)
+                add_into(other, 1, b, n, rgy)
+                c_fx(b, n, h).start()
+            forward_units(forward_full)
+            tail_units(0, forward_half)
+            tail_units(1, lambda b, n, h: c_fx(b, n, h).start())
 
             @pl.when(jnp.logical_not(last))
             def _():
@@ -459,9 +478,9 @@
             @pl.when(k > 0)
             def _():
                 for t in range(2):
-                    loop(0, E, lambda b: c_x(t, b).wait_send())
-                    for h in range(2):
-                        loop(E, NB, lambda b: c_x(t, b, h).wait_send())
+                    forward_units(lambda b, n, h: c_x(t, b, n, h).wait_send())
+                    for half in range(2):
+                        tail_units(half, lambda b, n, h: c_x(t, b, n, h).wait_send())
 
             for off in range(1, 4):
                 s_wait(par, off).wait_recv()
@@ -474,23 +493,12 @@
             def _():
                 pl.semaphore_wait(cr_x, 1)
 
-            def full(b, acc, halves):
-                if halves:
-                    c_a(b, 0).wait()
-                    c_a(b, 1).wait()
-                else:
-                    c_a(b).wait()
-                c_fy(b).wait_recv()
-                acc = update(0, b, None, ra, rfy, acc)
-                emit(0, b, None, last)
-                c_dy(b).wait_recv()
-                c_fx(b).wait_recv()
-                acc = update(1, b, None, rdy, rfx, acc)
-                emit(1, b, None, last)
-                return acc
-
-            acc = lax.fori_loop(0, G, lambda b, acc: full(b, acc, True), jnp.zeros((8, VECS), jnp.float32))
-            acc = lax.fori_loop(G, E, lambda b, acc: full(b, acc, False), acc)
+            for half in range(2):
+                lead_units(half, lambda b, n, h: c_a(b, n, h).wait())
+            units(G, NB, UA_HOME, lambda b: c_a(b, UA_HOME).wait())
+            units(0, NB, UD, lambda b: c_dy(b).wait_recv())
+            acc = lax.fori_loop(
+                0, E // UF, lambda u, acc: finish(u * UF, UF, None, last, acc), jnp.zeros((8, VECS), jnp.float32))
             sacc[...] = acc
 
             @pl.when(jnp.logical_not(last))
@@ -509,18 +517,20 @@
 
     @pl.when(home)
     def _():
-        def close(b, h):
-            o_local(row, b, h).wait()
-            o_remote(1 - row, b, h).wait_send()
-        loop(0, E, lambda b: close(b, None))
-        for h in range(2):
-            loop(E, NB, lambda b: close(b, h))
+        def close(b, n, h):
+            o_local(row, b, n, h).wait()
+            o_remote(1 - row, b, n, h).wait_send()
+        forward_units(close)
+        for half in range(2):
+            tail_units(half, close)
 
     @pl.when(away)
     def _():
-        loop(0, E, lambda b: o_remote(1 - row, b, None).wait_recv())
-        for h in range(2):
-            loop(E, NB, lambda b: o_remote(1 - row, b, h).wait_recv())
+        def close(b, n, h):
+            o_remote(1 - row, b, n, h).wait_recv()
+        forward_units(close)
+        for half in range(2):
+            tail_units(half, close)
 
 
 def solution(mesh):
@@ -548,10 +558,10 @@
                 pltpu.VMEM((8, VECS), jnp.float32),
                 pltpu.VMEM((8, VECS), jnp.float32),
                 dma((RING,)), dma((X0C,)), dma((2,)), dma((2,)), dma((2,)), dma((X0C,)), dma((X0C,)),
-                dma((NB + G,)), dma((NB + G,)), dma((NB + G,)), dma((NB + G,)), dma((NB,)), dma((NB,)),
-                dma((NB + G,)), dma((NB + G,)), dma((NB + G,)), dma((NB + G,)),
-                dma((2 * (NB + G),)), dma((2 * (NB + G),)), dma((2, 4)), dma((2, 4)), dma, dma,
-                dma((NB + G,)), dma((NB + G,)), dma((NB + G,)),
+                dma((2 * NB,)), dma((2 * NB,)), dma((2 * NB,)), dma((2 * NB,)), dma((NB,)), dma((NB,)),
+                dma((2 * NB,)), dma((2 * NB,)), dma((2 * NB,)), dma((2 * NB,)),
+                dma((4 * NB,)), dma((4 * NB,)), dma((2, 4)), dma((2, 4)), dma, dma,
+                dma((2 * NB,)), dma((2 * NB,)), dma((2 * NB,)),
                 reg, reg, reg, reg, reg, reg,
             ],
             compiler_params=pltpu.CompilerParams(

time: 837 us -> 840 us (level)
  no operation moved by 1% of the time
where the time goes in v4:
time: 840 us
  Pallas kernels  836 us (100%)
    pallas_call x1, Pallas kernels, local_sweeps(): pl.pallas_call(kernel, name='sweeps', out_shape=jax.ShapeDtypeStruct((PIE...  836 us

profile of v4, /device:TPU:0, one launch (start us, length us, event | category | flops | bytes accessed | tf_op | source)
XLA Modules:
  0.0 839.7 jit_solution(11594043044825541841)
XLA Ops:
  0.0 835.9 %sweeps.1 = f32[3072,256]{1,0:T(8,128)} custom-call(bf16[12288,6144]{1,0:T(8,128)(2,1)} %a_hbm.1, f32[3072,256]{1,0:T(8,128)} %x_hbm.1, f32[3072,256]{1,0:T(8,128)} %v_hbm.1, s32[24,128]{1,0:T(8,128)} %bitcast.1), custom_call_target="tpu_custom_call" | custom-call | flops 309237645312 | bytes 1207959552 | tf_op jit(solution)/shard_map/sweeps/pallas_call | solution.py:542
  835.9 3.8 copy.6

commit v5 on v4

--- a/solution.py
+++ b/solution.py
@@ -20,13 +20,14 @@
 G = 4
 E = NB - G
 CH = 32
-LEAD = (1, 2)
-TAIL = (2, 2)
-UA_HOME = 4
-UA_AWAY = 2
-UG = 2
-UD = 6
-UF = 4
+LEAD = (1, 1)
+TAIL = (1, 1)
+UA_HOME = 1
+UA_AWAY = 1
+UG = 1
+UD = 1
+UF = 1
+HOLD = 24
 RING = 4
 X0C = 6
 X0R = PIECE // X0C
@@ -369,8 +370,12 @@
                     start(b - (size - 1), size)
 
             straight = jnp.logical_and(first, t == 0)
-            send_when(jnp.logical_and(straight, home), G, UA_HOME, lambda b, n: c_a(b, n).start())
+            held = n - HOLD + G
             send_when(jnp.logical_and(straight, away), 0, UA_AWAY, lambda b, n: c_a(b, n).start())
+
+            @pl.when(jnp.logical_and(jnp.logical_and(held >= G, held < NB), home))
+            def _():
+                c_a(held, 1).start()
             send_when(jnp.logical_and(jnp.logical_and(first, t == 1), away), G, UG, lambda b, n: c_gy(b, n).start())
             send_when(jnp.logical_and(jnp.logical_and(jnp.logical_not(first), t == 1), away), 0, UD,
                       lambda b, n: c_dy(b).start())

time: 840 us -> 838 us (level)
  no operation moved by 1% of the time
where the time goes in v5:
time: 838 us
  Pallas kernels  834 us (100%)
    pallas_call x1, Pallas kernels, local_sweeps(): pl.pallas_call(kernel, name='sweeps', out_shape=jax.ShapeDtypeStruct((PIE...  834 us

profile of v5, /device:TPU:0, one launch (start us, length us, event | category | flops | bytes accessed | tf_op | source)
XLA Modules:
  0.0 838.2 jit_solution(1351704209346888833)
XLA Ops:
  0.0 834.5 %sweeps.1 = f32[3072,256]{1,0:T(8,128)} custom-call(bf16[12288,6144]{1,0:T(8,128)(2,1)} %a_hbm.1, f32[3072,256]{1,0:T(8,128)} %x_hbm.1, f32[3072,256]{1,0:T(8,128)} %v_hbm.1, s32[24,128]{1,0:T(8,128)} %bitcast.1), custom_call_target="tpu_custom_call" | custom-call | flops 309237645312 | bytes 1207959552 | tf_op jit(solution)/shard_map/sweeps/pallas_call | solution.py:547
  834.5 3.8 copy.6

commit v6 on v5

--- a/solution.py
+++ b/solution.py
@@ -27,7 +27,7 @@
 UG = 1
 UD = 1
 UF = 1
-HOLD = 24
+HOLD = 16
 RING = 4
 X0C = 6
 X0R = PIECE // X0C
@@ -380,7 +380,12 @@
             send_when(jnp.logical_and(jnp.logical_and(jnp.logical_not(first), t == 1), away), 0, UD,
                       lambda b, n: c_dy(b).start())
 
-        loop(G, 4 * NB, rest)
+        loop(G, 2 * NB, rest)
+
+        @pl.when(home)
+        def _():
+            for half in range(2):
+                lead_units(half, lambda b, n, h: c_gy(b, n, h).wait_recv())
 
         def add_into(base, t, b, n, src):
             def step(c):
@@ -388,8 +393,58 @@
                 ybuf[at, :] = ybuf[at, :] + src[rows_of(b * BR + c * CH, CH), :]
             loop(0, n * BR // CH, step)
 
+        def forward_home(b):
+            @pl.when(b >= G)
+            def _():
+                c_gy(b, 1).wait_recv()
+            add_into(other, 1, b, 1, rgy)
+
+            @pl.when(b < E)
+            def _():
+                c_fx(b, 1).start()
+
+            @pl.when(b >= E)
+            def _():
+                c_fx(b, 1, 0).start()
+
+        def forward_away(b):
+            c_a(b, 1).wait()
+            add_into(same, 0, b, 1, ra)
+
+            @pl.when(b < E)
+            def _():
+                c_fy(b, 1).start()
+
+            @pl.when(b >= E)
+            def _():
+                c_fy(b, 1, 0).start()
+
+        def third(n):
+            rest(n)
+
+            @pl.when(home)
+            def _():
+                forward_home(n - 2 * NB)
+
+        def fourth(n):
+            rest(n)
+
+            @pl.when(away)
+            def _():
+                forward_away(n - 3 * NB)
+
+        loop(2 * NB, 3 * NB, third)
+
+        @pl.when(home)
+        def _():
+            tail_units(1, lambda b, n, h: c_fx(b, n, h).start())
+
+        loop(3 * NB, 4 * NB, fourth)
+
         @pl.when(away)
         def _away():
+            tail_units(1, lambda b, n, h: c_fy(b, n, h).start())
+
             @pl.when(k == 0)
             def _():
                 for c in range(X0C):
@@ -403,21 +458,6 @@
             def _():
                 first_mass()
                 s0_out.start()
-
-            def forward(b, n):
-                units(0, n, UA_AWAY, lambda i: c_a(b + i, UA_AWAY).wait())
-                add_into(same, 0, b, n, ra)
-
-            def forward_full(b, n, h):
-                forward(b, n)
-                c_fy(b, n).start()
-
-            def forward_half(b, n, h):
-                forward(b, n)
-                c_fy(b, n, h).start()
-            forward_units(forward_full)
-            tail_units(0, forward_half)
-            tail_units(1, lambda b, n, h: c_fy(b, n, h).start())
 
             @pl.when(jnp.logical_not(last))
             def _():
@@ -442,27 +482,6 @@
 
         @pl.when(home)
         def _home():
-            for half in range(2):
-                lead_units(half, lambda b, n, h: c_gy(b, n, h).wait_recv())
-
-            def arrived(b, n):
-                @pl.when(b >= G)
-                def _():
-                    units(0, n, UG, lambda i: c_gy(b + i, UG).wait_recv())
-
-            def forward_full(b, n, h):
-                arrived(b, n)
-                add_into(other, 1, b, n, rgy)
-                c_fx(b, n).start()
-
-            def forward_half(b, n, h):
-                arrived(b, n)
-                add_into(other, 1, b, n, rgy)
-                c_fx(b, n, h).start()
-            forward_units(forward_full)
-            tail_units(0, forward_half)
-            tail_units(1, lambda b, n, h: c_fx(b, n, h).start())
-
             @pl.when(jnp.logical_not(last))
             def _():
                 signal(cr_gy, yn)

time: 838 us -> 838 us (level)
  no operation moved by 1% of the time
where the time goes in v6:
time: 838 us
  Pallas kernels  834 us (100%)
    pallas_call x1, Pallas kernels, local_sweeps(): pl.pallas_call(kernel, name='sweeps', out_shape=jax.ShapeDtypeStruct((PIE...  834 us

profile of v6, /device:TPU:0, one launch (start us, length us, event | category | flops | bytes accessed | tf_op | source)
XLA Modules:
  0.0 838.2 jit_solution(774041029732306378)
XLA Ops:
  0.0 834.5 %sweeps.1 = f32[3072,256]{1,0:T(8,128)} custom-call(bf16[12288,6144]{1,0:T(8,128)(2,1)} %a_hbm.1, f32[3072,256]{1,0:T(8,128)} %x_hbm.1, f32[3072,256]{1,0:T(8,128)} %v_hbm.1, s32[24,128]{1,0:T(8,128)} %bitcast.1), custom_call_target="tpu_custom_call" | custom-call | flops 309237645312 | bytes 1207959552 | tf_op jit(solution)/shard_map/sweeps/pallas_call | solution.py:566
  834.5 3.8 copy.6

commit v7 on v6

--- a/solution.py
+++ b/solution.py
@@ -17,7 +17,7 @@
 COLS = 6144
 BR = 256
 NB = PIECE // BR
-G = 4
+G = 6
 E = NB - G
 CH = 32
 LEAD = (1, 1)
@@ -28,7 +28,7 @@
 UD = 1
 UF = 1
 HOLD = 16
-RING = 4
+RING = 6
 X0C = 6
 X0R = PIECE // X0C
 

time: 838 us -> 838 us (level)
  no operation moved by 1% of the time
where the time goes in v7:
time: 838 us
  Pallas kernels  834 us (100%)
    pallas_call x1, Pallas kernels, local_sweeps(): pl.pallas_call(kernel, name='sweeps', out_shape=jax.ShapeDtypeStruct((PIE...  834 us

profile of v7, /device:TPU:0, one launch (start us, length us, event | category | flops | bytes accessed | tf_op | source)
XLA Modules:
  0.0 838.0 jit_solution(17688784533749609365)
XLA Ops:
  0.0 834.2 %sweeps.1 = f32[3072,256]{1,0:T(8,128)} custom-call(bf16[12288,6144]{1,0:T(8,128)(2,1)} %a_hbm.1, f32[3072,256]{1,0:T(8,128)} %x_hbm.1, f32[3072,256]{1,0:T(8,128)} %v_hbm.1, s32[24,128]{1,0:T(8,128)} %bitcast.1), custom_call_target="tpu_custom_call" | custom-call | flops 309237645312 | bytes 1207959552 | tf_op jit(solution)/shard_map/sweeps/pallas_call | solution.py:566
  834.2 3.8 copy.6

commit v8 on v5

--- a/solution.py
+++ b/solution.py
@@ -27,7 +27,7 @@
 UG = 1
 UD = 1
 UF = 1
-HOLD = 24
+HOLD = 36
 RING = 4
 X0C = 6
 X0R = PIECE // X0C

time: 838 us -> 838 us (level)
  no operation moved by 1% of the time
where the time goes in v8:
time: 838 us
  Pallas kernels  834 us (100%)
    pallas_call x1, Pallas kernels, local_sweeps(): pl.pallas_call(kernel, name='sweeps', out_shape=jax.ShapeDtypeStruct((PIE...  834 us

profile of v8, /device:TPU:0, one launch (start us, length us, event | category | flops | bytes accessed | tf_op | source)
XLA Modules:
  0.0 838.2 jit_solution(5241203060584986606)
XLA Ops:
  0.0 834.5 %sweeps.1 = f32[3072,256]{1,0:T(8,128)} custom-call(bf16[12288,6144]{1,0:T(8,128)(2,1)} %a_hbm.1, f32[3072,256]{1,0:T(8,128)} %x_hbm.1, f32[3072,256]{1,0:T(8,128)} %v_hbm.1, s32[24,128]{1,0:T(8,128)} %bitcast.1), custom_call_target="tpu_custom_call" | custom-call | flops 309237645312 | bytes 1207959552 | tf_op jit(solution)/shard_map/sweeps/pallas_call | solution.py:547
  834.5 3.8 copy.6

commit v9 on v6

--- a/solution.py
+++ b/solution.py
@@ -23,7 +23,7 @@
 LEAD = (1, 1)
 TAIL = (1, 1)
 UA_HOME = 1
-UA_AWAY = 1
+UA_AWAY = 4
 UG = 1
 UD = 1
 UF = 1
@@ -408,7 +408,9 @@
                 c_fx(b, 1, 0).start()
 
         def forward_away(b):
-            c_a(b, 1).wait()
+            @pl.when(lax.rem(b, UA_AWAY) == 0)
+            def _():
+                c_a(b, UA_AWAY).wait()
             add_into(same, 0, b, 1, ra)
 
             @pl.when(b < E)

time: 838 us -> 869 us (1.037)
  Pallas kernels: 834 us -> 866 us
    pallas_call x1, Pallas kernels: 834 us -> 866 us  [local_sweeps(): pl.pallas_call(kernel, name='sweeps', out_shape=jax.ShapeDtypeStruct((PIE...]
where the time goes in v9:
time: 869 us
  Pallas kernels  866 us (100%)
    pallas_call x1, Pallas kernels, local_sweeps(): pl.pallas_call(kernel, name='sweeps', out_shape=jax.ShapeDtypeStruct((PIE...  866 us

profile of v9, /device:TPU:0, one launch (start us, length us, event | category | flops | bytes accessed | tf_op | source)
XLA Modules:
  0.0 869.3 jit_solution(17357983024627809408)
XLA Ops:
  0.0 865.5 %sweeps.1 = f32[3072,256]{1,0:T(8,128)} custom-call(bf16[12288,6144]{1,0:T(8,128)(2,1)} %a_hbm.1, f32[3072,256]{1,0:T(8,128)} %x_hbm.1, f32[3072,256]{1,0:T(8,128)} %v_hbm.1, s32[24,128]{1,0:T(8,128)} %bitcast.1), custom_call_target="tpu_custom_call" | custom-call | flops 309237645312 | bytes 1207959552 | tf_op jit(solution)/shard_map/sweeps/pallas_call | solution.py:568
  865.5 3.8 copy.6

commit v10 on v6

--- a/solution.py
+++ b/solution.py
@@ -27,7 +27,6 @@
 UG = 1
 UD = 1
 UF = 1
-HOLD = 16
 RING = 4
 X0C = 6
 X0R = PIECE // X0C
@@ -183,16 +182,17 @@
 
     def s_copy(par, off):
         dst_col = lax.rem(col + off, 4)
-        return remote(sbuf.at[par, col], sbuf.at[par, col], s_s.at[par, off], s_r.at[par, col],
+        return remote(sbuf.at[par, col, pl.ds(0, 1)], sbuf.at[par, col, pl.ds(0, 1)], s_s.at[par, off], s_r.at[par, col],
                       (dst_col, lax.div(dst_col, 2)))
 
     def s_wait(par, off):
         src_col = lax.rem(col + off, 4)
-        return remote(sbuf.at[par, src_col], sbuf.at[par, src_col], s_s.at[par, off], s_r.at[par, src_col],
+        return remote(sbuf.at[par, src_col, pl.ds(0, 1)], sbuf.at[par, src_col, pl.ds(0, 1)], s_s.at[par, off],
+                      s_r.at[par, src_col],
                       (src_col, lax.div(src_col, 2)))
 
     def s_publish(par, value):
-        sbuf[par, col] = value
+        sbuf[par, col, 0:1, :] = jnp.sum(value, axis=0, keepdims=True)
         for off in range(1, 4):
             s_copy(par, off).start()
 
@@ -265,18 +265,18 @@
             0, G // n, lambda u, acc: finish(E + u * n, n, h, last, acc), jnp.zeros((8, HALF), jnp.float32))
         sacc[:, cols(h)] = sacc[:, cols(h)] + part
 
-    def drain_forward():
+    def drain_forward(keep):
         @pl.when(home)
         def _():
             forward_units(lambda b, n, h: c_fx(b, n, h).wait_send())
             for half in range(2):
-                tail_units(half, lambda b, n, h: c_fx(b, n, h).wait_send())
+                loop(NB - 1 if half and keep else E, NB, lambda b: c_fx(b, 1, half).wait_send())
 
         @pl.when(away)
         def _():
             forward_units(lambda b, n, h: c_fy(b, n, h).wait_send())
             for half in range(2):
-                tail_units(half, lambda b, n, h: c_fy(b, n, h).wait_send())
+                loop(NB - 1 if half and keep else E, NB, lambda b: c_fy(b, 1, half).wait_send())
 
     def sweep(k, carry):
         last = k == SWEEPS - 1
@@ -310,16 +310,29 @@
                 if h == 1:
                     fetch(n + RING)
                 size = LEAD[h]
-                whole = lax.rem(n, size) == size - 1
-                b = n - (size - 1)
-
-                @pl.when(jnp.logical_and(whole, home))
+                ready = n >= (1 if h == 0 else 0)
+
+                @pl.when(jnp.logical_and(home, ready))
                 def _():
-                    c_a(b, size, h).start()
-
-                @pl.when(jnp.logical_and(whole, away))
+                    if h == 0:
+                        @pl.when(n == 1)
+                        def _():
+                            @pl.when(k > 0)
+                            def _():
+                                loop(E, NB - 1, lambda b: c_fx(b, 1, 1).wait_send())
+                            c_a(0, 1, h).start()
+                    c_a(n, 1, h).start()
+
+                @pl.when(jnp.logical_and(away, ready))
                 def _():
-                    c_gy(b, size, h).start()
+                    if h == 0:
+                        @pl.when(n == 1)
+                        def _():
+                            @pl.when(k > 0)
+                            def _():
+                                loop(E, NB - 1, lambda b: c_fy(b, 1, 1).wait_send())
+                            c_gy(0, 1, h).start()
+                    c_gy(n, 1, h).start()
             loop(0, G, one)
 
         lead(0)
@@ -342,7 +355,7 @@
 
         @pl.when(k > 0)
         def _():
-            drain_forward()
+            drain_forward(True)
 
             @pl.when(home)
             def _():
@@ -370,12 +383,7 @@
                     start(b - (size - 1), size)
 
             straight = jnp.logical_and(first, t == 0)
-            held = n - HOLD + G
-            send_when(jnp.logical_and(straight, away), 0, UA_AWAY, lambda b, n: c_a(b, n).start())
-
-            @pl.when(jnp.logical_and(jnp.logical_and(held >= G, held < NB), home))
-            def _():
-                c_a(held, 1).start()
+            send_when(straight, 0, 1, lambda b, n: c_a(b, n).start())
             send_when(jnp.logical_and(jnp.logical_and(first, t == 1), away), G, UG, lambda b, n: c_gy(b, n).start())
             send_when(jnp.logical_and(jnp.logical_and(jnp.logical_not(first), t == 1), away), 0, UD,
                       lambda b, n: c_dy(b).start())
@@ -509,8 +517,8 @@
             for off in range(1, 4):
                 s_wait(par, off).wait_recv()
                 s_copy(par, off).wait_send()
-            total = (sbuf[par, 0] + sbuf[par, 1]) + (sbuf[par, 2] + sbuf[par, 3])
-            mass = jnp.sum(total, axis=0, keepdims=True) / VERTS
+            part = [sbuf[par, c, 0:1, :] for c in range(4)]
+            mass = ((part[0] + part[1]) + (part[2] + part[3])) / VERTS
             coef[...] = jnp.broadcast_to(DAMPING * mass + (1.0 - DAMPING), (8, VECS))
 
             @pl.when(jnp.logical_not(last))
@@ -537,7 +545,7 @@
     @pl.when(home)
     def _():
         finish_half(1, jnp.bool_(True))
-    drain_forward()
+    drain_forward(False)
 
     @pl.when(home)
     def _():

time: 838 us -> 839 us (level)
  no operation moved by 1% of the time
where the time goes in v10:
time: 839 us
  Pallas kernels  835 us (100%)
    pallas_call x1, Pallas kernels, local_sweeps(): pl.pallas_call(kernel, name='sweeps', out_shape=jax.ShapeDtypeStruct((PIE...  835 us

profile of v10, /device:TPU:0, one launch (start us, length us, event | category | flops | bytes accessed | tf_op | source)
XLA Modules:
  0.0 839.1 jit_solution(13674814745697170983)
XLA Ops:
  0.0 835.3 %sweeps.1 = f32[3072,256]{1,0:T(8,128)} custom-call(bf16[12288,6144]{1,0:T(8,128)(2,1)} %a_hbm.1, f32[3072,256]{1,0:T(8,128)} %x_hbm.1, f32[3072,256]{1,0:T(8,128)} %v_hbm.1, s32[24,128]{1,0:T(8,128)} %bitcast.1), custom_call_target="tpu_custom_call" | custom-call | flops 309237645312 | bytes 1207959552 | tf_op jit(solution)/shard_map/sweeps/pallas_call | solution.py:574
  835.3 3.8 copy.6

commit v11 on v3

v11 whole, which is shorter than its diff:
```python
import jax
import jax.numpy as jnp
from jax import lax
from jax.experimental import pallas as pl
from jax.experimental.pallas import tpu as pltpu
from jax.sharding import PartitionSpec as P

SWEEPS = 8
DAMPING = 0.85
MESH = pl.DeviceIdType.MESH

VERTS = 24576
VECS = 256
HALF = 128
PIECE = 3072
ROWS = 12288
COLS = 6144
BR = 256
NB = PIECE // BR
G = 4
E = NB - G
CH = 32
RING = 4
X0C = 6
X0R = PIECE // X0C


def kernel(a_hbm, x_hbm, v_hbm, d_hbm, out_hbm,
           abuf, xbf, ybuf, ra, rgy, rdy, rfx, rfy, vbuf, dbuf, dint, sbuf, s0buf, coef, sacc,
           a_sem, xin_sem, in_sem, ina_s, ina_r, x0_s, x0_r,
           a_s, a_r, gy_s, gy_r, dy_s, dy_r, fx_s, fx_r, fy_s, fy_r,
           x_s, x_r, s_s, s_r, s0_s, s0_r, o_l, o_s, o_r,
           cr_hh1, cr_hh2, cr_hw, cr_gy, cr_ww, cr_x):
    col = lax.axis_index('col')
    row = lax.axis_index('row')
    cx, cy = lax.rem(col, 2), lax.div(col, 2)
    home = row == cy
    away = jnp.logical_not(home)
    xn = (cy * 2 + 1 - cx, row)
    yn = ((1 - cy) * 2 + cx, row)
    mate = (col, 1 - row)
    same = cx * COLS
    other = (1 - cx) * COLS
    mine = row * PIECE
    far = (1 - row) * PIECE

    def rows_of(start, size):
        return pl.ds(pl.multiple_of(start, size), size)

    def blocks(start, b, n):
        return pl.ds(pl.multiple_of(start + b * BR, BR), n * BR)

    def cols(h):
        return pl.ds(0, VECS) if h is None else pl.ds(h * HALF, HALF)

    def remote(src, dst, send, recv, dev):
        return pltpu.make_async_remote_copy(
            src_ref=src, dst_ref=dst, send_sem=send, recv_sem=recv, device_id=dev, device_id_type=MESH)

    def loop(lo, hi, body):
        def step(i, c):
            body(i)
            return c
        lax.fori_loop(lo, hi, step, 0)

    def signal(sem, dev):
        pl.semaphore_signal(sem, inc=1, device_id=dev, device_id_type=MESH)

    def x_in(c):
        return pltpu.make_async_copy(x_hbm.at[rows_of(c * X0R, X0R)], vbuf.at[rows_of(mine + c * X0R, X0R)], xin_sem.at[c])

    for c in range(X0C):
        x_in(c).start()

    barrier = pltpu.get_barrier_semaphore()
    for off in range(4):
        for r in range(2):
            if off == 0 and r == 1:
                continue
            signal(barrier, (lax.rem(col + off, 4), row if r == 0 and off else 1 - row))

    def flow(start, b, n, h, dst, send, recv, dev, late):
        i = b if h != 1 else NB + b - (E if late else 0)
        return remote(ybuf.at[blocks(start, b, n), cols(h)], dst.at[blocks(0, b, n), cols(h)], send, recv.at[i], dev)

    def c_a(b, h=None, n=1):
        return flow(other, b, n, h, ra, a_s, a_r, xn, False)

    def c_gy(b, h=None, n=1):
        return flow(other + PIECE, b, n, h, rgy, gy_s, gy_r, yn, False)

    def c_dy(b, n=1):
        return remote(ybuf.at[blocks(same + PIECE, b, n)], rdy.at[blocks(0, b, n)], dy_s, dy_r, yn)

    def c_fx(b, h=None, n=1):
        return flow(other + PIECE, b, n, h, rfx, fx_s, fx_r, xn, True)

    def c_fy(b, h=None, n=1):
        return flow(same, b, n, h, rfy, fy_s, fy_r, yn, True)

    def c_x(t, b, h=None):
        at = blocks(t * PIECE, b, 1)
        return remote(xbf.at[at, cols(h)], xbf.at[at, cols(h)], x_s, x_r.at[1 if h == 1 else 0], mate)

    def x_bytes(rows, i):
        return remote(xbf.at[pl.ds(0, rows)], xbf.at[pl.ds(0, rows)], x_s, x_r.at[i], mate)

    def block_of(n):
        m = n - G
        pair = m < 2 * E
        t0 = jnp.where(pair, lax.rem(m, 2), 1)
        b0 = jnp.where(pair, jnp.where(t0 == 0, G, 0) + lax.div(m, 2), m - E)
        b0 = jnp.where(m < 0, n, b0)
        t0 = jnp.where(jnp.logical_xor(home, jnp.logical_or(m < 0, t0 == 0)), 1, 0)
        m = n - 2 * NB
        first = n < 2 * NB
        t = jnp.where(first, t0, 1 - lax.div(m, NB))
        b = jnp.where(first, b0, lax.rem(m, NB))
        return jnp.where(first, other, same) + t * PIECE + b * BR

    def a_copy(n):
        slot = lax.rem(n, RING)
        return pltpu.make_async_copy(a_hbm.at[rows_of(block_of(n), BR)], abuf.at[slot], a_sem.at[slot])

    d_in = pltpu.make_async_copy(d_hbm, dint.at[row], in_sem.at[0])
    v_in = pltpu.make_async_copy(v_hbm, vbuf.at[rows_of(mine, PIECE)], in_sem.at[1])
    v_out = remote(v_hbm, vbuf.at[rows_of(mine, PIECE)], ina_s.at[0], ina_r.at[0], mate)
    d_out = remote(d_hbm, dint.at[row], ina_s.at[1], ina_r.at[1], mate)
    s0_out = remote(s0buf.at[row], s0buf.at[row], s0_s, s0_r, mate)

    def x0_copy(start, c, n=1):
        at = pl.ds(pl.multiple_of(start + c * X0R, X0R), n * X0R)
        return remote(xbf.at[at], xbf.at[at], x0_s, x0_r, mate)

    for c in range(X0C):
        x_in(c).wait()

        def convert(i, c=c):
            at = rows_of(mine + c * X0R + i * CH, CH)
            xbf[at, :] = vbuf[at, :].astype(jnp.bfloat16)
        loop(0, X0R // CH, convert)
        if c == 0:
            pl.semaphore_wait(barrier, 7)
        x0_copy(mine, c).start()
        if c < RING:
            a_copy(jnp.int32(c)).start()
    d_in.start()

    @pl.when(away)
    def _():
        d_out.start()
        v_out.start()

    x0_copy(far, 0, X0C).wait_recv()

    def s_copy(par, off):
        dst_col = lax.rem(col + off, 4)
        return remote(sbuf.at[par, col], sbuf.at[par, col], s_s.at[par], s_r.at[par], (dst_col, lax.div(dst_col, 2)))

    def s_bytes(par):
        return remote(sbuf.at[par, pl.ds(0, 3)], sbuf.at[par, pl.ds(0, 3)], s_s.at[par], s_r.at[par], mate)

    def s_publish(par, value):
        sbuf[par, col] = jnp.sum(value, axis=0, keepdims=True)
        for off in range(1, 4):
            s_copy(par, off).start()

    def spread(r):
        def group(g):
            flags = dint[r, pl.ds(g, 1), :].astype(jnp.float32)
            dbuf[rows_of(r * PIECE + g * 128, 128), :] = jnp.broadcast_to(flags, (128, 128)).T.astype(jnp.bfloat16)
        loop(0, PIECE // 128, group)

    def flags(start, h):
        d = dbuf[rows_of(start, CH), :].astype(jnp.float32)
        return d if h is not None else jnp.concatenate([d, d], axis=1)

    def fold(w):
        return jnp.sum(w.reshape(CH // 8, 8, w.shape[1]), axis=0)

    def first_mass():
        d_in.wait()
        spread(row)

        def add(c, acc):
            at = mine + c * CH
            return acc + fold(vbuf[rows_of(at, CH), :] * flags(at, None))
        s0buf[row] = lax.fori_loop(0, PIECE // CH, add, jnp.zeros((8, VECS), jnp.float32))

    def update(t, b, h, one, two, acc):
        def step(c, acc):
            at = rows_of(same + t * PIECE + b * BR + c * CH, CH)
            own = rows_of(t * PIECE + b * BR + c * CH, CH)
            there = rows_of(b * BR + c * CH, CH)
            y = (ybuf[at, cols(h)] + one[there, cols(h)]) + two[there, cols(h)]
            cf = jnp.concatenate([coef[:, cols(h)]] * (CH // 8), axis=0)
            x = DAMPING * y + cf * vbuf[own, cols(h)]
            xbf[own, cols(h)] = x.astype(jnp.bfloat16)
            ybuf[at, cols(h)] = x
            return acc + fold(x * flags(t * PIECE + b * BR + c * CH, h))
        return lax.fori_loop(0, BR // CH, step, acc)

    def o_local(t, b, h=None, n=1):
        return pltpu.make_async_copy(
            ybuf.at[blocks(same + t * PIECE, b, n), cols(h)], out_hbm.at[blocks(0, b, n), cols(h)], o_l)

    def o_remote(t, b, h=None, n=1):
        return remote(ybuf.at[blocks(same + t * PIECE, b, n), cols(h)], out_hbm.at[blocks(0, b, n), cols(h)], o_s, o_r, mate)

    def emit(t, b, h, last):
        @pl.when(jnp.logical_not(last))
        def _():
            c_x(t, b, h).start()

        @pl.when(jnp.logical_and(last, row == t))
        def _():
            o_local(t, b, h).start()

        @pl.when(jnp.logical_and(last, row != t))
        def _():
            o_remote(t, b, h).start()

    def finish(b, h, last, acc):
        c_fy(b, h).wait_recv()
        acc = update(0, b, h, ra, rfy, acc)
        emit(0, b, h, last)
        c_fx(b, h).wait_recv()
        acc = update(1, b, h, rdy, rfx, acc)
        emit(1, b, h, last)
        return acc

    def finish_half(h, last):
        part = lax.fori_loop(E, NB, lambda b, acc: finish(b, h, last, acc), jnp.zeros((8, HALF), jnp.float32))
        sacc[:, cols(h)] = sacc[:, cols(h)] + part

    def drain_forward():
        @pl.when(home)
        def _():
            c_fx(0, n=NB).wait_send()

        @pl.when(away)
        def _():
            c_fy(0, n=NB).wait_send()

    def sweep(k, carry):
        last = k == SWEEPS - 1
        more = jnp.logical_not(last)
        par = lax.rem(k, 2)

        def multiply(n, h):
            start = block_of(n)
            ybuf[rows_of(start, BR), cols(h)] = jnp.dot(
                abuf[lax.rem(n, RING)], xbf[:, cols(h)], preferred_element_type=jnp.float32)

        def fetch(n):
            @pl.when(jnp.logical_not(jnp.logical_and(last, n >= 4 * NB)))
            def _():
                a_copy(lax.rem(n, 4 * NB)).start()

        @pl.when(k > 0)
        def _():
            @pl.when(home)
            def _():
                pl.semaphore_wait(cr_hh1, 1)

            @pl.when(away)
            def _():
                pl.semaphore_wait(cr_gy, 1)

        def lead(h):
            def one(n):
                if h == 0:
                    a_copy(n).wait()
                multiply(n, h)
                if h == 1:
                    fetch(n + RING)

                @pl.when(home)
                def _():
                    c_a(n, h).start()

                @pl.when(away)
                def _():
                    c_gy(n, h).start()
            loop(0, G, one)

        lead(0)

        @pl.when(k > 0)
        def _():
            @pl.when(home)
            def _():
                finish_half(1, jnp.bool_(False))
                s_publish(par, sacc[...])
                signal(cr_hh2, xn)
                signal(cr_hw, yn)

            @pl.when(away)
            def _():
                x_bytes(G * BR, 1).wait_recv()

        lead(1)

        @pl.when(k > 0)
        def _():
            drain_forward()

            @pl.when(home)
            def _():
                pl.semaphore_wait(cr_hh2, 1)

            @pl.when(away)
            def _():
                pl.semaphore_wait(cr_ww, 1)
                pl.semaphore_wait(cr_hw, 1)

        def step(n):
            a_copy(n).wait()
            multiply(n, None)
            fetch(n + RING)
            at = block_of(n) - jnp.where(n < 2 * NB, other, same)
            return lax.div(at, PIECE), lax.div(lax.rem(at, PIECE), BR)

        def part_one(n):
            t, b = step(n)

            @pl.when(t == 0)
            def _():
                c_a(b).start()

            @pl.when(jnp.logical_and(t == 1, away))
            def _():
                c_gy(b).start()
        loop(G, 2 * NB, part_one)

        @pl.when(k == 0)
        def _():
            first_mass()

            @pl.when(away)
            def _():
                s0_out.start()

            @pl.when(home)
            def _():
                v_in.start()
                remote(d_hbm, dint.at[1 - row], ina_s.at[1], ina_r.at[1], mate).wait_recv()
                remote(s0buf.at[1 - row], s0buf.at[1 - row], s0_s, s0_r, mate).wait_recv()
                s_publish(0, s0buf[0] + s0buf[1])

        def add_into(start, b, src):
            def add(c):
                at = rows_of(start + b * BR + c * CH, CH)
                ybuf[at, :] = ybuf[at, :] + src[rows_of(b * BR + c * CH, CH), :]
            loop(0, BR // CH, add)

        def send_on(copy, b):
            @pl.when(b < E)
            def _():
                copy(b).start()

            @pl.when(b >= E)
            def _():
                copy(b, 0).start()

        def part_two(n):
            b = n - 2 * NB
            step(n)

            @pl.when(away)
            def _():
                c_dy(b).start()

            @pl.when(home)
            def _():
                @pl.when(b < G)
                def _():
                    c_gy(b, 0).wait_recv()
                    c_gy(b, 1).wait_recv()

                @pl.when(b >= G)
                def _():
                    c_gy(b).wait_recv()
                add_into(other + PIECE, b, rgy)
                send_on(c_fx, b)
        loop(2 * NB, 3 * NB, part_two)

        @pl.when(home)
        def _():
            loop(E, NB, lambda b: c_fx(b, 1).start())

        def part_three(n):
            b = n - 3 * NB
            step(n)

            @pl.when(away)
            def _():
                c_a(b).wait_recv()
                add_into(same, b, ra)
                send_on(c_fy, b)
        loop(3 * NB, 4 * NB, part_three)

        @pl.when(away)
        def _away():
            loop(E, NB, lambda b: c_fy(b, 1).start())

            @pl.when(k == 0)
            def _():
                x0_copy(mine, 0, X0C).wait_send()
                v_out.wait_send()
                d_out.wait_send()
                s0_out.wait_send()

            @pl.when(more)
            def _():
                signal(cr_x, mate)
                signal(cr_ww, xn)
            c_a(0, n=NB).wait_send()
            c_gy(0, n=NB).wait_send()
            c_dy(0, NB).wait_send()

            @pl.when(more)
            def _():
                x_bytes(2 * PIECE - G * BR, 0).wait_recv()

        @pl.when(home)
        def _home():
            @pl.when(more)
            def _():
                signal(cr_gy, yn)

            @pl.when(k == 0)
            def _():
                spread(1 - row)
                x0_copy(mine, 0, X0C).wait_send()
                remote(v_hbm, vbuf.at[rows_of(far, PIECE)], ina_s.at[0], ina_r.at[0], mate).wait_recv()
                v_in.wait()

            @pl.when(k > 0)
            def _():
                x_bytes(2 * PIECE, 0).wait_send()

            s_bytes(par).wait_recv()
            s_bytes(par).wait_send()
            mass = ((sbuf[par, 0] + sbuf[par, 1]) + (sbuf[par, 2] + sbuf[par, 3])) / VERTS
            coef[...] = jnp.broadcast_to(DAMPING * mass + (1.0 - DAMPING), (8, VECS))

            @pl.when(more)
            def _():
                pl.semaphore_wait(cr_x, 1)

            c_a(0, n=NB).wait_send()
            for h in range(2):
                loop(0, G, lambda b: c_a(b, h).wait_recv())
            loop(G, NB, lambda b: c_a(b).wait_recv())
            c_dy(0, NB).wait_recv()
            sacc[...] = lax.fori_loop(0, E, lambda b, acc: finish(b, None, last, acc), jnp.zeros((8, VECS), jnp.float32))

            @pl.when(more)
            def _():
                signal(cr_hh1, xn)
            finish_half(0, last)

        return carry

    lax.fori_loop(0, SWEEPS, sweep, 0)

    @pl.when(home)
    def _():
        finish_half(1, jnp.bool_(True))
    drain_forward()

    @pl.when(home)
    def _():
        o_local(row, 0, n=NB).wait()
        o_remote(1 - row, 0, n=NB).wait_send()

    @pl.when(away)
    def _():
        o_remote(1 - row, 0, n=NB).wait_recv()


def solution(mesh):
    dma = pltpu.SemaphoreType.DMA
    reg = pltpu.SemaphoreType.REGULAR

    def local_sweeps(mat_tile, x_piece, tele_piece, dang_piece):
        part = pltpu.VMEM((PIECE, VECS), jnp.float32)
        return pl.pallas_call(
            kernel,
            name="sweeps",
            out_shape=jax.ShapeDtypeStruct((PIECE, VECS), jnp.float32),
            in_specs=[pl.BlockSpec(memory_space=pl.ANY)] * 4,
            out_specs=pl.BlockSpec(memory_space=pl.ANY),
            scratch_shapes=[
                pltpu.VMEM((RING, BR, COLS), jnp.bfloat16),
                pltpu.VMEM((COLS, VECS), jnp.bfloat16),
                pltpu.VMEM((ROWS, VECS), jnp.float32),
                part, part, part, part, part,
                pltpu.VMEM((COLS, VECS), jnp.float32),
                pltpu.VMEM((COLS, 128), jnp.bfloat16),
                pltpu.VMEM((2, PIECE // 128, 128), jnp.int32),
                pltpu.VMEM((2, 4, 1, VECS), jnp.float32),
                pltpu.VMEM((2, 8, VECS), jnp.float32),
                pltpu.VMEM((8, VECS), jnp.float32),
                pltpu.VMEM((8, VECS), jnp.float32),
                dma((RING,)), dma((X0C,)), dma((2,)), dma((2,)), dma((2,)), dma, dma,
                dma, dma((NB + G,)), dma, dma((NB + G,)), dma, dma, dma, dma((NB + G,)), dma, dma((NB + G,)),
                dma, dma((2,)), dma((2,)), dma((2,)), dma, dma, dma, dma, dma,
                reg, reg, reg, reg, reg, reg,
            ],
            compiler_params=pltpu.CompilerParams(
                collective_id=0, has_side_effects=True, vmem_limit_bytes=67_000_000),
            cost_estimate=pl.CostEstimate(
                flops=2 * ROWS * COLS * VECS * SWEEPS, bytes_accessed=2 * ROWS * COLS * SWEEPS, transcendentals=0),
        )(mat_tile, x_piece, tele_piece, dang_piece.reshape(PIECE // 128, 128))

    vec_spec = P(('col', 'row'), None)
    return jax.shard_map(local_sweeps, mesh=mesh,
                         in_specs=(P('row', 'col'), vec_spec, vec_spec, P(('col', 'row'))),
                         out_specs=vec_spec, check_vma=False)
```

time: 837 us -> 826 us (0.987)
  Pallas kernels: 833 us -> 822 us
    pallas_call x1, Pallas kernels: 833 us -> 822 us  [local_sweeps(): pl.pallas_call(kernel, name='sweeps', out_shape=jax.ShapeDtypeStruct((PIE...]
where the time goes in v11:
time: 826 us
  Pallas kernels  822 us (100%)
    pallas_call x1, Pallas kernels, local_sweeps(): pl.pallas_call(kernel, name='sweeps', out_shape=jax.ShapeDtypeStruct((PIE...  822 us

profile of v11, /device:TPU:0, one launch (start us, length us, event | category | flops | bytes accessed | tf_op | source)
XLA Modules:
  0.0 825.6 jit_solution(13470725287967335447)
XLA Ops:
  0.0 821.8 %sweeps.1 = f32[3072,256]{1,0:T(8,128)} custom-call(bf16[12288,6144]{1,0:T(8,128)(2,1)} %a_hbm.1, f32[3072,256]{1,0:T(8,128)} %x_hbm.1, f32[3072,256]{1,0:T(8,128)} %v_hbm.1, s32[24,128]{1,0:T(8,128)} %bitcast.1), custom_call_target="tpu_custom_call" | custom-call | flops 309237645312 | bytes 1207959552 | tf_op jit(solution)/shard_map/sweeps/pallas_call | solution.py:489
  821.8 3.8 copy.6

commit v12 on v11

--- a/solution.py
+++ b/solution.py
@@ -25,11 +25,11 @@
 X0R = PIECE // X0C
 
 
-def kernel(a_hbm, x_hbm, v_hbm, d_hbm, out_hbm,
+def kernel(a_hbm, x_hbm, v_hbm, d_hbm, out,
            abuf, xbf, ybuf, ra, rgy, rdy, rfx, rfy, vbuf, dbuf, dint, sbuf, s0buf, coef, sacc,
            a_sem, xin_sem, in_sem, ina_s, ina_r, x0_s, x0_r,
            a_s, a_r, gy_s, gy_r, dy_s, dy_r, fx_s, fx_r, fy_s, fy_r,
-           x_s, x_r, s_s, s_r, s0_s, s0_r, o_l, o_s, o_r,
+           x_s, x_r, s_s, s_r, s0_s, s0_r, o_s, o_r,
            cr_hh1, cr_hh2, cr_hw, cr_gy, cr_ww, cr_x):
     col = lax.axis_index('col')
     row = lax.axis_index('row')
@@ -200,12 +200,14 @@
             return acc + fold(x * flags(t * PIECE + b * BR + c * CH, h))
         return lax.fori_loop(0, BR // CH, step, acc)
 
-    def o_local(t, b, h=None, n=1):
-        return pltpu.make_async_copy(
-            ybuf.at[blocks(same + t * PIECE, b, n), cols(h)], out_hbm.at[blocks(0, b, n), cols(h)], o_l)
+    def keep(t, b, h):
+        def step(c):
+            there = rows_of(b * BR + c * CH, CH)
+            out[there, cols(h)] = ybuf[rows_of(same + t * PIECE + b * BR + c * CH, CH), cols(h)]
+        loop(0, BR // CH, step)
 
     def o_remote(t, b, h=None, n=1):
-        return remote(ybuf.at[blocks(same + t * PIECE, b, n), cols(h)], out_hbm.at[blocks(0, b, n), cols(h)], o_s, o_r, mate)
+        return remote(ybuf.at[blocks(same + t * PIECE, b, n), cols(h)], out.at[blocks(0, b, n), cols(h)], o_s, o_r, mate)
 
     def emit(t, b, h, last):
         @pl.when(jnp.logical_not(last))
@@ -214,7 +216,7 @@
 
         @pl.when(jnp.logical_and(last, row == t))
         def _():
-            o_local(t, b, h).start()
+            keep(t, b, h)
 
         @pl.when(jnp.logical_and(last, row != t))
         def _():
@@ -472,7 +474,6 @@
 
     @pl.when(home)
     def _():
-        o_local(row, 0, n=NB).wait()
         o_remote(1 - row, 0, n=NB).wait_send()
 
     @pl.when(away)
@@ -483,6 +484,9 @@
 def solution(mesh):
     dma = pltpu.SemaphoreType.DMA
     reg = pltpu.SemaphoreType.REGULAR
+
+    def in_hbm(a):
+        return pltpu.with_memory_space_constraint(a, pltpu.HBM)
 
     def local_sweeps(mat_tile, x_piece, tele_piece, dang_piece):
         part = pltpu.VMEM((PIECE, VECS), jnp.float32)
@@ -490,8 +494,8 @@
             kernel,
             name="sweeps",
             out_shape=jax.ShapeDtypeStruct((PIECE, VECS), jnp.float32),
-            in_specs=[pl.BlockSpec(memory_space=pl.ANY)] * 4,
-            out_specs=pl.BlockSpec(memory_space=pl.ANY),
+            in_specs=[pl.BlockSpec(memory_space=pltpu.HBM)] * 4,
+            out_specs=pl.BlockSpec(memory_space=pltpu.VMEM),
             scratch_shapes=[
                 pltpu.VMEM((RING, BR, COLS), jnp.bfloat16),
                 pltpu.VMEM((COLS, VECS), jnp.bfloat16),
@@ -506,14 +510,14 @@
                 pltpu.VMEM((8, VECS), jnp.float32),
                 dma((RING,)), dma((X0C,)), dma((2,)), dma((2,)), dma((2,)), dma, dma,
                 dma, dma((NB + G,)), dma, dma((NB + G,)), dma, dma, dma, dma((NB + G,)), dma, dma((NB + G,)),
-                dma, dma((2,)), dma((2,)), dma((2,)), dma, dma, dma, dma, dma,
+                dma, dma((2,)), dma((2,)), dma((2,)), dma, dma, dma, dma,
                 reg, reg, reg, reg, reg, reg,
             ],
             compiler_params=pltpu.CompilerParams(
-                collective_id=0, has_side_effects=True, vmem_limit_bytes=67_000_000),
+                collective_id=0, has_side_effects=True, vmem_limit_bytes=53_300_000),
             cost_estimate=pl.CostEstimate(
                 flops=2 * ROWS * COLS * VECS * SWEEPS, bytes_accessed=2 * ROWS * COLS * SWEEPS, transcendentals=0),
-        )(mat_tile, x_piece, tele_piece, dang_piece.reshape(PIECE // 128, 128))
+        )(mat_tile, x_piece, tele_piece, in_hbm(dang_piece.reshape(PIECE // 128, 128)))
 
     vec_spec = P(('col', 'row'), None)
     return jax.shard_map(local_sweeps, mesh=mesh,

time: 826 us -> 824 us (level)
  no operation moved by 1% of the time
where the time goes in v12:
time: 824 us
  Pallas kernels  822 us (100%)
    pallas_call x1, Pallas kernels, local_sweeps(): pl.pallas_call(kernel, name='sweeps', out_shape=jax.ShapeDtypeStruct((PIE...  822 us

profile of v12, /device:TPU:0, one launch (start us, length us, event | category | flops | bytes accessed | tf_op | source)
XLA Modules:
  0.0 823.6 jit_solution(1035034352585408827)
XLA Ops:
  0.0 821.9 %sweeps.1 = f32[3072,256]{1,0:T(8,128)S(1)} custom-call(bf16[12288,6144]{1,0:T(8,128)(2,1)} %a_hbm.1, f32[3072,256]{1,0:T(8,128)} %x_hbm.1, f32[3072,256]{1,0:T(8,128)} %v_hbm.1, s32[24,128]{1,0:T(8,128)} %bitcast.1), custom_call_target="tpu_custom_call" | custom-call | flops 309237645312 | bytes 1207959552 | tf_op jit(solution)/shard_map/sweeps/pallas_call | solution.py:493
  821.9 1.7 copy.6

commit v13 on v12

--- a/solution.py
+++ b/solution.py
@@ -21,16 +21,15 @@
 E = NB - G
 CH = 32
 RING = 4
-X0C = 6
+X0C = 4
 X0R = PIECE // X0C
 
 
 def kernel(a_hbm, x_hbm, v_hbm, d_hbm, out,
            abuf, xbf, ybuf, ra, rgy, rdy, rfx, rfy, vbuf, dbuf, dint, sbuf, s0buf, coef, sacc,
-           a_sem, xin_sem, in_sem, ina_s, ina_r, x0_s, x0_r,
+           a_sem, in_sem, x0_s, x0_r,
            a_s, a_r, gy_s, gy_r, dy_s, dy_r, fx_s, fx_r, fy_s, fy_r,
-           x_s, x_r, s_s, s_r, s0_s, s0_r, o_s, o_r,
-           cr_hh1, cr_hh2, cr_hw, cr_gy, cr_ww, cr_x):
+           x_s, x_r, s_s, s_r, o_s, o_r, cr_0, cr_1, cr_2):
     col = lax.axis_index('col')
     row = lax.axis_index('row')
     cx, cy = lax.rem(col, 2), lax.div(col, 2)
@@ -67,7 +66,7 @@
         pl.semaphore_signal(sem, inc=1, device_id=dev, device_id_type=MESH)
 
     def x_in(c):
-        return pltpu.make_async_copy(x_hbm.at[rows_of(c * X0R, X0R)], vbuf.at[rows_of(mine + c * X0R, X0R)], xin_sem.at[c])
+        return pltpu.make_async_copy(x_hbm.at[rows_of(c * X0R, X0R)], vbuf.at[rows_of(mine + c * X0R, X0R)], in_sem.at[c])
 
     for c in range(X0C):
         x_in(c).start()
@@ -79,24 +78,40 @@
                 continue
             signal(barrier, (lax.rem(col + off, 4), row if r == 0 and off else 1 - row))
 
-    def flow(start, b, n, h, dst, send, recv, dev, late):
-        i = b if h != 1 else NB + b - (E if late else 0)
+    def flow(start, b, n, h, dst, send, recv, i, dev):
         return remote(ybuf.at[blocks(start, b, n), cols(h)], dst.at[blocks(0, b, n), cols(h)], send, recv.at[i], dev)
 
     def c_a(b, h=None, n=1):
-        return flow(other, b, n, h, ra, a_s, a_r, xn, False)
+        return flow(other, b, n, h, ra, a_s, a_r, lax.div(b, G), xn)
 
     def c_gy(b, h=None, n=1):
-        return flow(other + PIECE, b, n, h, rgy, gy_s, gy_r, yn, False)
+        return flow(other + PIECE, b, n, h, rgy, gy_s, gy_r, lax.div(b, G), yn)
 
     def c_dy(b, n=1):
         return remote(ybuf.at[blocks(same + PIECE, b, n)], rdy.at[blocks(0, b, n)], dy_s, dy_r, yn)
 
+    def late(b, h):
+        return lax.div(b, G) if h is None else E // G + 2 * h + jnp.where(b == NB - 1, 1, 0)
+
     def c_fx(b, h=None, n=1):
-        return flow(other + PIECE, b, n, h, rfx, fx_s, fx_r, xn, True)
+        return flow(other + PIECE, b, n, h, rfx, fx_s, fx_r, late(b, h), xn)
 
     def c_fy(b, h=None, n=1):
-        return flow(same, b, n, h, rfy, fy_s, fy_r, yn, True)
+        return flow(same, b, n, h, rfy, fy_s, fy_r, late(b, h), yn)
+
+    def arrived(copy, b, h):
+        if h is None:
+            @pl.when(lax.rem(b, G) == 0)
+            def _():
+                copy(b, n=G).wait_recv()
+        else:
+            @pl.when(b == E)
+            def _():
+                copy(b, h, n=G - 1).wait_recv()
+
+            @pl.when(b == NB - 1)
+            def _():
+                copy(b, h).wait_recv()
 
     def c_x(t, b, h=None):
         at = blocks(t * PIECE, b, 1)
@@ -124,9 +139,15 @@
 
     d_in = pltpu.make_async_copy(d_hbm, dint.at[row], in_sem.at[0])
     v_in = pltpu.make_async_copy(v_hbm, vbuf.at[rows_of(mine, PIECE)], in_sem.at[1])
-    v_out = remote(v_hbm, vbuf.at[rows_of(mine, PIECE)], ina_s.at[0], ina_r.at[0], mate)
-    d_out = remote(d_hbm, dint.at[row], ina_s.at[1], ina_r.at[1], mate)
-    s0_out = remote(s0buf.at[row], s0buf.at[row], s0_s, s0_r, mate)
+
+    def v_copy(r):
+        return remote(v_hbm, vbuf.at[rows_of(r * PIECE, PIECE)], fx_s, x_r.at[0], mate)
+
+    def d_copy(r):
+        return remote(d_hbm, dint.at[r], x_s, x_r.at[1], mate)
+
+    def s0_copy(r):
+        return remote(s0buf.at[r], s0buf.at[r], o_s, o_r, mate)
 
     def x0_copy(start, c, n=1):
         at = pl.ds(pl.multiple_of(start + c * X0R, X0R), n * X0R)
@@ -148,17 +169,39 @@
 
     @pl.when(away)
     def _():
-        d_out.start()
-        v_out.start()
-
+        d_copy(row).start()
+        v_copy(row).start()
+
+    def half_product(n, start):
+        at = rows_of(start, PIECE)
+        return jnp.dot(abuf[lax.rem(n, RING), :, at], xbf[at, :], preferred_element_type=jnp.float32)
+
+    def first_own(n):
+        a_copy(n).wait()
+        ybuf[rows_of(block_of(n), BR), :] = half_product(n, mine)
+    loop(0, G, first_own)
     x0_copy(far, 0, X0C).wait_recv()
+
+    def first_far(n):
+        at = rows_of(block_of(n), BR)
+        ybuf[at, :] = ybuf[at, :] + half_product(n, far)
+        a_copy(n + RING).start()
+        for h in range(2):
+            @pl.when(home)
+            def _():
+                c_a(n, h).start()
+
+            @pl.when(away)
+            def _():
+                c_gy(n, h).start()
+    loop(0, G, first_far)
 
     def s_copy(par, off):
         dst_col = lax.rem(col + off, 4)
-        return remote(sbuf.at[par, col], sbuf.at[par, col], s_s.at[par], s_r.at[par], (dst_col, lax.div(dst_col, 2)))
+        return remote(sbuf.at[par, col], sbuf.at[par, col], s_s, s_r.at[par], (dst_col, lax.div(dst_col, 2)))
 
     def s_bytes(par):
-        return remote(sbuf.at[par, pl.ds(0, 3)], sbuf.at[par, pl.ds(0, 3)], s_s.at[par], s_r.at[par], mate)
+        return remote(sbuf.at[par, pl.ds(0, 3)], sbuf.at[par, pl.ds(0, 3)], s_s, s_r.at[par], mate)
 
     def s_publish(par, value):
         sbuf[par, col] = jnp.sum(value, axis=0, keepdims=True)
@@ -223,10 +266,10 @@
             o_remote(t, b, h).start()
 
     def finish(b, h, last, acc):
-        c_fy(b, h).wait_recv()
+        arrived(c_fy, b, h)
         acc = update(0, b, h, ra, rfy, acc)
         emit(0, b, h, last)
-        c_fx(b, h).wait_recv()
+        arrived(c_fx, b, h)
         acc = update(1, b, h, rdy, rfx, acc)
         emit(1, b, h, last)
         return acc
@@ -258,16 +301,6 @@
             @pl.when(jnp.logical_not(jnp.logical_and(last, n >= 4 * NB)))
             def _():
                 a_copy(lax.rem(n, 4 * NB)).start()
-
-        @pl.when(k > 0)
-        def _():
-            @pl.when(home)
-            def _():
-                pl.semaphore_wait(cr_hh1, 1)
-
-            @pl.when(away)
-            def _():
-                pl.semaphore_wait(cr_gy, 1)
 
         def lead(h):
             def one(n):
@@ -286,35 +319,29 @@
                     c_gy(n, h).start()
             loop(0, G, one)
 
-        lead(0)
-
         @pl.when(k > 0)
-        def _():
+        def _head():
+            pl.semaphore_wait(cr_0, 1)
+            lead(0)
+
             @pl.when(home)
             def _():
                 finish_half(1, jnp.bool_(False))
                 s_publish(par, sacc[...])
-                signal(cr_hh2, xn)
-                signal(cr_hw, yn)
+                signal(cr_1, xn)
+                signal(cr_1, yn)
 
             @pl.when(away)
             def _():
                 x_bytes(G * BR, 1).wait_recv()
 
-        lead(1)
-
-        @pl.when(k > 0)
-        def _():
+            lead(1)
             drain_forward()
-
-            @pl.when(home)
-            def _():
-                pl.semaphore_wait(cr_hh2, 1)
+            pl.semaphore_wait(cr_1, 1)
 
             @pl.when(away)
             def _():
-                pl.semaphore_wait(cr_ww, 1)
-                pl.semaphore_wait(cr_hw, 1)
+                pl.semaphore_wait(cr_2, 1)
 
         def step(n):
             a_copy(n).wait()
@@ -341,13 +368,13 @@
 
             @pl.when(away)
             def _():
-                s0_out.start()
+                s0_copy(row).start()
 
             @pl.when(home)
             def _():
                 v_in.start()
-                remote(d_hbm, dint.at[1 - row], ina_s.at[1], ina_r.at[1], mate).wait_recv()
-                remote(s0buf.at[1 - row], s0buf.at[1 - row], s0_s, s0_r, mate).wait_recv()
+                d_copy(1 - row).wait_recv()
+                s0_copy(1 - row).wait_recv()
                 s_publish(0, s0buf[0] + s0buf[1])
 
         def add_into(start, b, src):
@@ -375,14 +402,9 @@
 
             @pl.when(home)
             def _():
-                @pl.when(b < G)
+                @pl.when(lax.rem(b, G) == 0)
                 def _():
-                    c_gy(b, 0).wait_recv()
-                    c_gy(b, 1).wait_recv()
-
-                @pl.when(b >= G)
-                def _():
-                    c_gy(b).wait_recv()
+                    c_gy(b, n=G).wait_recv()
                 add_into(other + PIECE, b, rgy)
                 send_on(c_fx, b)
         loop(2 * NB, 3 * NB, part_two)
@@ -397,7 +419,9 @@
 
             @pl.when(away)
             def _():
-                c_a(b).wait_recv()
+                @pl.when(lax.rem(b, G) == 0)
+                def _():
+                    c_a(b, n=G).wait_recv()
                 add_into(same, b, ra)
                 send_on(c_fy, b)
         loop(3 * NB, 4 * NB, part_three)
@@ -409,14 +433,14 @@
             @pl.when(k == 0)
             def _():
                 x0_copy(mine, 0, X0C).wait_send()
-                v_out.wait_send()
-                d_out.wait_send()
-                s0_out.wait_send()
+                v_copy(row).wait_send()
+                d_copy(row).wait_send()
+                s0_copy(row).wait_send()
 
             @pl.when(more)
             def _():
-                signal(cr_x, mate)
-                signal(cr_ww, xn)
+                signal(cr_2, mate)
+                signal(cr_2, xn)
             c_a(0, n=NB).wait_send()
             c_gy(0, n=NB).wait_send()
             c_dy(0, NB).wait_send()
@@ -429,13 +453,13 @@
         def _home():
             @pl.when(more)
             def _():
-                signal(cr_gy, yn)
+                signal(cr_0, yn)
 
             @pl.when(k == 0)
             def _():
                 spread(1 - row)
                 x0_copy(mine, 0, X0C).wait_send()
-                remote(v_hbm, vbuf.at[rows_of(far, PIECE)], ina_s.at[0], ina_r.at[0], mate).wait_recv()
+                v_copy(1 - row).wait_recv()
                 v_in.wait()
 
             @pl.when(k > 0)
@@ -449,18 +473,17 @@
 
             @pl.when(more)
             def _():
-                pl.semaphore_wait(cr_x, 1)
+                pl.semaphore_wait(cr_2, 1)
 
             c_a(0, n=NB).wait_send()
-            for h in range(2):
-                loop(0, G, lambda b: c_a(b, h).wait_recv())
-            loop(G, NB, lambda b: c_a(b).wait_recv())
+            for b in range(0, NB, G):
+                c_a(b, n=G).wait_recv()
             c_dy(0, NB).wait_recv()
             sacc[...] = lax.fori_loop(0, E, lambda b, acc: finish(b, None, last, acc), jnp.zeros((8, VECS), jnp.float32))
 
             @pl.when(more)
             def _():
-                signal(cr_hh1, xn)
+                signal(cr_0, xn)
             finish_half(0, last)
 
         return carry
@@ -508,10 +531,9 @@
                 pltpu.VMEM((2, 8, VECS), jnp.float32),
                 pltpu.VMEM((8, VECS), jnp.float32),
                 pltpu.VMEM((8, VECS), jnp.float32),
-                dma((RING,)), dma((X0C,)), dma((2,)), dma((2,)), dma((2,)), dma, dma,
-                dma, dma((NB + G,)), dma, dma((NB + G,)), dma, dma, dma, dma((NB + G,)), dma, dma((NB + G,)),
-                dma, dma((2,)), dma((2,)), dma((2,)), dma, dma, dma, dma,
-                reg, reg, reg, reg, reg, reg,
+                dma((RING,)), dma((X0C,)), dma, dma,
+                dma, dma((NB // G,)), dma, dma((NB // G,)), dma, dma, dma, dma((E // G + 4,)), dma, dma((E // G + 4,)),
+                dma, dma((2,)), dma, dma((2,)), dma, dma, reg, reg, reg,
             ],
             compiler_params=pltpu.CompilerParams(
                 collective_id=0, has_side_effects=True, vmem_limit_bytes=53_300_000),

time: 824 us -> 825 us (level)
  no operation moved by 1% of the time
where the time goes in v13:
time: 825 us
  Pallas kernels  823 us (100%)
    pallas_call x1, Pallas kernels, local_sweeps(): pl.pallas_call(kernel, name='sweeps', out_shape=jax.ShapeDtypeStruct((PIE...  823 us

profile of v13, /device:TPU:0, one launch (start us, length us, event | category | flops | bytes accessed | tf_op | source)
XLA Modules:
  0.0 824.9 jit_solution(16325904590102208821)
XLA Ops:
  0.0 823.3 %sweeps.1 = f32[3072,256]{1,0:T(8,128)S(1)} custom-call(bf16[12288,6144]{1,0:T(8,128)(2,1)} %a_hbm.1, f32[3072,256]{1,0:T(8,128)} %x_hbm.1, f32[3072,256]{1,0:T(8,128)} %v_hbm.1, s32[24,128]{1,0:T(8,128)} %bitcast.1), custom_call_target="tpu_custom_call" | custom-call | flops 309237645312 | bytes 1207959552 | tf_op jit(solution)/shard_map/sweeps/pallas_call | solution.py:516
  823.3 1.7 copy.6

commit v14 on v13

--- a/solution.py
+++ b/solution.py
@@ -23,6 +23,7 @@
 RING = 4
 X0C = 4
 X0R = PIECE // X0C
+EARLY = 2
 
 
 def kernel(a_hbm, x_hbm, v_hbm, d_hbm, out,
@@ -179,22 +180,32 @@
     def first_own(n):
         a_copy(n).wait()
         ybuf[rows_of(block_of(n), BR), :] = half_product(n, mine)
-    loop(0, G, first_own)
+    loop(0, EARLY, first_own)
     x0_copy(far, 0, X0C).wait_recv()
+
+    def first_send(n):
+        a_copy(n + RING).start()
+        for h in range(2):
+            @pl.when(home)
+            def _():
+                c_a(n, h).start()
+
+            @pl.when(away)
+            def _():
+                c_gy(n, h).start()
 
     def first_far(n):
         at = rows_of(block_of(n), BR)
         ybuf[at, :] = ybuf[at, :] + half_product(n, far)
-        a_copy(n + RING).start()
-        for h in range(2):
-            @pl.when(home)
-            def _():
-                c_a(n, h).start()
-
-            @pl.when(away)
-            def _():
-                c_gy(n, h).start()
-    loop(0, G, first_far)
+        first_send(n)
+    loop(0, EARLY, first_far)
+
+    def first_whole(n):
+        a_copy(n).wait()
+        ybuf[rows_of(block_of(n), BR), :] = jnp.dot(
+            abuf[lax.rem(n, RING)], xbf[...], preferred_element_type=jnp.float32)
+        first_send(n)
+    loop(EARLY, G, first_whole)
 
     def s_copy(par, off):
         dst_col = lax.rem(col + off, 4)

time: 825 us -> 823 us (level)
  no operation moved by 1% of the time
where the time goes in v14:
time: 823 us
  Pallas kernels  821 us (100%)
    pallas_call x1, Pallas kernels, local_sweeps(): pl.pallas_call(kernel, name='sweeps', out_shape=jax.ShapeDtypeStruct((PIE...  821 us

profile of v14, /device:TPU:0, one launch (start us, length us, event | category | flops | bytes accessed | tf_op | source)
XLA Modules:
  0.0 823.1 jit_solution(8649328765984237148)
XLA Ops:
  0.0 821.4 %sweeps.1 = f32[3072,256]{1,0:T(8,128)S(1)} custom-call(bf16[12288,6144]{1,0:T(8,128)(2,1)} %a_hbm.1, f32[3072,256]{1,0:T(8,128)} %x_hbm.1, f32[3072,256]{1,0:T(8,128)} %v_hbm.1, s32[24,128]{1,0:T(8,128)} %bitcast.1), custom_call_target="tpu_custom_call" | custom-call | flops 309237645312 | bytes 1207959552 | tf_op jit(solution)/shard_map/sweeps/pallas_call | solution.py:527
  821.4 1.7 copy.6

commit v15 on v13

--- a/solution.py
+++ b/solution.py
@@ -149,9 +149,9 @@
     def s0_copy(r):
         return remote(s0buf.at[r], s0buf.at[r], o_s, o_r, mate)
 
-    def x0_copy(start, c, n=1):
+    def x0_copy(start, c, h, n=1):
         at = pl.ds(pl.multiple_of(start + c * X0R, X0R), n * X0R)
-        return remote(xbf.at[at], xbf.at[at], x0_s, x0_r, mate)
+        return remote(xbf.at[at, cols(h)], xbf.at[at, cols(h)], x0_s, x0_r.at[1 if h == 1 else 0], mate)
 
     for c in range(X0C):
         x_in(c).wait()
@@ -162,39 +162,17 @@
         loop(0, X0R // CH, convert)
         if c == 0:
             pl.semaphore_wait(barrier, 7)
-        x0_copy(mine, c).start()
+        x0_copy(mine, c, 0).start()
         if c < RING:
             a_copy(jnp.int32(c)).start()
+    for c in range(X0C):
+        x0_copy(mine, c, 1).start()
     d_in.start()
 
     @pl.when(away)
     def _():
         d_copy(row).start()
         v_copy(row).start()
-
-    def half_product(n, start):
-        at = rows_of(start, PIECE)
-        return jnp.dot(abuf[lax.rem(n, RING), :, at], xbf[at, :], preferred_element_type=jnp.float32)
-
-    def first_own(n):
-        a_copy(n).wait()
-        ybuf[rows_of(block_of(n), BR), :] = half_product(n, mine)
-    loop(0, G, first_own)
-    x0_copy(far, 0, X0C).wait_recv()
-
-    def first_far(n):
-        at = rows_of(block_of(n), BR)
-        ybuf[at, :] = ybuf[at, :] + half_product(n, far)
-        a_copy(n + RING).start()
-        for h in range(2):
-            @pl.when(home)
-            def _():
-                c_a(n, h).start()
-
-            @pl.when(away)
-            def _():
-                c_gy(n, h).start()
-    loop(0, G, first_far)
 
     def s_copy(par, off):
         dst_col = lax.rem(col + off, 4)
@@ -319,23 +297,33 @@
                     c_gy(n, h).start()
             loop(0, G, one)
 
+        @pl.when(k == 0)
+        def _():
+            x0_copy(far, 0, 0, X0C).wait_recv()
+
         @pl.when(k > 0)
-        def _head():
+        def _():
             pl.semaphore_wait(cr_0, 1)
-            lead(0)
-
-            @pl.when(home)
-            def _():
-                finish_half(1, jnp.bool_(False))
-                s_publish(par, sacc[...])
-                signal(cr_1, xn)
-                signal(cr_1, yn)
-
-            @pl.when(away)
-            def _():
-                x_bytes(G * BR, 1).wait_recv()
-
-            lead(1)
+        lead(0)
+
+        @pl.when(k == 0)
+        def _():
+            x0_copy(far, 0, 1, X0C).wait_recv()
+
+        @pl.when(jnp.logical_and(k > 0, home))
+        def _():
+            finish_half(1, jnp.bool_(False))
+            s_publish(par, sacc[...])
+            signal(cr_1, xn)
+            signal(cr_1, yn)
+
+        @pl.when(jnp.logical_and(k > 0, away))
+        def _():
+            x_bytes(G * BR, 1).wait_recv()
+        lead(1)
+
+        @pl.when(k > 0)
+        def _():
             drain_forward()
             pl.semaphore_wait(cr_1, 1)
 
@@ -432,7 +420,7 @@
 
             @pl.when(k == 0)
             def _():
-                x0_copy(mine, 0, X0C).wait_send()
+                x0_copy(mine, 0, None, X0C).wait_send()
                 v_copy(row).wait_send()
                 d_copy(row).wait_send()
                 s0_copy(row).wait_send()
@@ -458,7 +446,7 @@
             @pl.when(k == 0)
             def _():
                 spread(1 - row)
-                x0_copy(mine, 0, X0C).wait_send()
+                x0_copy(mine, 0, None, X0C).wait_send()
                 v_copy(1 - row).wait_recv()
                 v_in.wait()
 
@@ -531,7 +519,7 @@
                 pltpu.VMEM((2, 8, VECS), jnp.float32),
                 pltpu.VMEM((8, VECS), jnp.float32),
                 pltpu.VMEM((8, VECS), jnp.float32),
-                dma((RING,)), dma((X0C,)), dma, dma,
+                dma((RING,)), dma((X0C,)), dma, dma((2,)),
                 dma, dma((NB // G,)), dma, dma((NB // G,)), dma, dma, dma, dma((E // G + 4,)), dma, dma((E // G + 4,)),
                 dma, dma((2,)), dma, dma((2,)), dma, dma, reg, reg, reg,
             ],

time: 825 us -> 822 us (level)
  no operation moved by 1% of the time
where the time goes in v15:
time: 822 us
  Pallas kernels  820 us (100%)
    pallas_call x1, Pallas kernels, local_sweeps(): pl.pallas_call(kernel, name='sweeps', out_shape=jax.ShapeDtypeStruct((PIE...  820 us

profile of v15, /device:TPU:0, one launch (start us, length us, event | category | flops | bytes accessed | tf_op | source)
XLA Modules:
  0.0 822.0 jit_solution(8009066418811352944)
XLA Ops:
  0.0 820.3 %sweeps.1 = f32[3072,256]{1,0:T(8,128)S(1)} custom-call(bf16[12288,6144]{1,0:T(8,128)(2,1)} %a_hbm.1, f32[3072,256]{1,0:T(8,128)} %x_hbm.1, f32[3072,256]{1,0:T(8,128)} %v_hbm.1, s32[24,128]{1,0:T(8,128)} %bitcast.1), custom_call_target="tpu_custom_call" | custom-call | flops 309237645312 | bytes 1207959552 | tf_op jit(solution)/shard_map/sweeps/pallas_call | solution.py:504
  820.3 1.7 copy.6

commit v16 on v15

--- a/solution.py
+++ b/solution.py
@@ -29,7 +29,7 @@
            abuf, xbf, ybuf, ra, rgy, rdy, rfx, rfy, vbuf, dbuf, dint, sbuf, s0buf, coef, sacc,
            a_sem, in_sem, x0_s, x0_r,
            a_s, a_r, gy_s, gy_r, dy_s, dy_r, fx_s, fx_r, fy_s, fy_r,
-           x_s, x_r, s_s, s_r, o_s, o_r, cr_0, cr_1, cr_2):
+           x_s, x_r, s_s, s_r, o_s, o_r, held_r, cr_0, cr_1, cr_2):
     col = lax.axis_index('col')
     row = lax.axis_index('row')
     cx, cy = lax.rem(col, 2), lax.div(col, 2)
@@ -90,6 +90,12 @@
     def c_dy(b, n=1):
         return remote(ybuf.at[blocks(same + PIECE, b, n)], rdy.at[blocks(0, b, n)], dy_s, dy_r, yn)
 
+    def held_a():
+        return remote(ybuf.at[blocks(other, NB - 1, 1)], ra.at[blocks(0, NB - 1, 1)], a_s, held_r, xn)
+
+    def held_dy():
+        return remote(ybuf.at[blocks(same + PIECE, NB - 1, 1)], rdy.at[blocks(0, NB - 1, 1)], dy_s, held_r, yn)
+
     def late(b, h):
         return lax.div(b, G) if h is None else E // G + 2 * h + jnp.where(b == NB - 1, 1, 0)
 
@@ -256,6 +262,31 @@
         part = lax.fori_loop(E, NB, lambda b, acc: finish(b, h, last, acc), jnp.zeros((8, HALF), jnp.float32))
         sacc[:, cols(h)] = sacc[:, cols(h)] + part
 
+    def finish_last():
+        def piece(t, b, h):
+            arrived(c_fy if t == 0 else c_fx, b, h)
+            result(t, b, h)
+
+        def result(t, b, h):
+            update(t, b, h, ra if t == 0 else rdy, rfy if t == 0 else rfx, jnp.zeros((8, HALF), jnp.float32))
+            emit(t, b, h, jnp.bool_(True))
+
+        for kept in range(2):
+            @pl.when(row == kept)
+            def _():
+                end = jnp.int32(NB - 1)
+                for h in range(2):
+                    def both(b):
+                        piece(1 - kept, b, h)
+                        piece(kept, b, h)
+                    loop(E, NB - 1, both)
+                    piece(1 - kept, end, h)
+                for h in range(2):
+                    arrived(c_fy if kept == 0 else c_fx, end, h)
+                (held_a() if kept == 0 else held_dy()).wait_recv()
+                for h in range(2):
+                    result(kept, end, h)
+
     def drain_forward():
         @pl.when(home)
         def _():
@@ -269,6 +300,8 @@
         last = k == SWEEPS - 1
         more = jnp.logical_not(last)
         par = lax.rem(k, 2)
+        hold_a = jnp.logical_and(jnp.logical_and(last, home), row == 0)
+        hold_dy = jnp.logical_and(last, row == 1)
 
         def multiply(n, h):
             start = block_of(n)
@@ -341,7 +374,7 @@
         def part_one(n):
             t, b = step(n)
 
-            @pl.when(t == 0)
+            @pl.when(jnp.logical_and(t == 0, jnp.logical_not(jnp.logical_and(hold_a, b == NB - 1))))
             def _():
                 c_a(b).start()
 
@@ -384,7 +417,7 @@
             b = n - 2 * NB
             step(n)
 
-            @pl.when(away)
+            @pl.when(jnp.logical_and(away, jnp.logical_not(jnp.logical_and(hold_dy, b == NB - 1))))
             def _():
                 c_dy(b).start()
 
@@ -401,6 +434,10 @@
         def _():
             loop(E, NB, lambda b: c_fx(b, 1).start())
 
+            @pl.when(hold_a)
+            def _():
+                held_a().start()
+
         def part_three(n):
             b = n - 3 * NB
             step(n)
@@ -418,6 +455,10 @@
         def _away():
             loop(E, NB, lambda b: c_fy(b, 1).start())
 
+            @pl.when(hold_dy)
+            def _():
+                held_dy().start()
+
             @pl.when(k == 0)
             def _():
                 x0_copy(mine, 0, None, X0C).wait_send()
@@ -463,28 +504,47 @@
             def _():
                 pl.semaphore_wait(cr_2, 1)
 
-            c_a(0, n=NB).wait_send()
-            for b in range(0, NB, G):
+            @pl.when(more)
+            def _():
+                c_a(0, n=NB).wait_send()
+            for b in range(0, E, G):
                 c_a(b, n=G).wait_recv()
-            c_dy(0, NB).wait_recv()
+
+            @pl.when(hold_a)
+            def _():
+                c_a(E, n=G - 1).wait_recv()
+
+            @pl.when(jnp.logical_not(hold_a))
+            def _():
+                c_a(E, n=G).wait_recv()
+
+            @pl.when(hold_dy)
+            def _():
+                c_dy(0, NB - 1).wait_recv()
+
+            @pl.when(jnp.logical_not(hold_dy))
+            def _():
+                c_dy(0, NB).wait_recv()
             sacc[...] = lax.fori_loop(0, E, lambda b, acc: finish(b, None, last, acc), jnp.zeros((8, VECS), jnp.float32))
 
             @pl.when(more)
             def _():
                 signal(cr_0, xn)
-            finish_half(0, last)
+                finish_half(0, jnp.bool_(False))
+
+            @pl.when(last)
+            def _():
+                finish_last()
 
         return carry
 
     lax.fori_loop(0, SWEEPS, sweep, 0)
+
+    drain_forward()
 
     @pl.when(home)
     def _():
-        finish_half(1, jnp.bool_(True))
-    drain_forward()
-
-    @pl.when(home)
-    def _():
+        c_a(0, n=NB).wait_send()
         o_remote(1 - row, 0, n=NB).wait_send()
 
     @pl.when(away)
@@ -521,7 +581,7 @@
                 pltpu.VMEM((8, VECS), jnp.float32),
                 dma((RING,)), dma((X0C,)), dma, dma((2,)),
                 dma, dma((NB // G,)), dma, dma((NB // G,)), dma, dma, dma, dma((E // G + 4,)), dma, dma((E // G + 4,)),
-                dma, dma((2,)), dma, dma((2,)), dma, dma, reg, reg, reg,
+                dma, dma((2,)), dma, dma((2,)), dma, dma, dma, reg, reg, reg,
             ],
             compiler_params=pltpu.CompilerParams(
                 collective_id=0, has_side_effects=True, vmem_limit_bytes=53_300_000),

time: 822 us -> 821 us (level)
  no operation moved by 1% of the time
where the time goes in v16:
time: 821 us
  Pallas kernels  819 us (100%)
    pallas_call x1, Pallas kernels, local_sweeps(): pl.pallas_call(kernel, name='sweeps', out_shape=jax.ShapeDtypeStruct((PIE...  819 us

profile of v16, /device:TPU:0, one launch (start us, length us, event | category | flops | bytes accessed | tf_op | source)
XLA Modules:
  0.0 821.1 jit_solution(17176390842832294372)
XLA Ops:
  0.0 819.4 %sweeps.1 = f32[3072,256]{1,0:T(8,128)S(1)} custom-call(bf16[12288,6144]{1,0:T(8,128)(2,1)} %a_hbm.1, f32[3072,256]{1,0:T(8,128)} %x_hbm.1, f32[3072,256]{1,0:T(8,128)} %v_hbm.1, s32[24,128]{1,0:T(8,128)} %bitcast.1), custom_call_target="tpu_custom_call" | custom-call | flops 309237645312 | bytes 1207959552 | tf_op jit(solution)/shard_map/sweeps/pallas_call | solution.py:564
  819.4 1.7 copy.6

commit v17 on v16

--- a/solution.py
+++ b/solution.py
@@ -21,7 +21,7 @@
 E = NB - G
 CH = 32
 RING = 4
-X0C = 4
+X0C = 3
 X0R = PIECE // X0C
 
 
@@ -65,11 +65,12 @@
     def signal(sem, dev):
         pl.semaphore_signal(sem, inc=1, device_id=dev, device_id_type=MESH)
 
-    def x_in(c):
-        return pltpu.make_async_copy(x_hbm.at[rows_of(c * X0R, X0R)], vbuf.at[rows_of(mine + c * X0R, X0R)], in_sem.at[c])
+    def x_in(c, h):
+        return pltpu.make_async_copy(x_hbm.at[rows_of(c * X0R, X0R), cols(h)], vbuf.at[rows_of(mine + c * X0R, X0R), cols(h)],
+                                     in_sem.at[h * X0C + c])
 
     for c in range(X0C):
-        x_in(c).start()
+        x_in(c, 0).start()
 
     barrier = pltpu.get_barrier_semaphore()
     for off in range(4):
@@ -159,20 +160,43 @@
         at = pl.ds(pl.multiple_of(start + c * X0R, X0R), n * X0R)
         return remote(xbf.at[at, cols(h)], xbf.at[at, cols(h)], x0_s, x0_r.at[1 if h == 1 else 0], mate)
 
+    a_copy(jnp.int32(0)).start()
     for c in range(X0C):
-        x_in(c).wait()
-
-        def convert(i, c=c):
-            at = rows_of(mine + c * X0R + i * CH, CH)
-            xbf[at, :] = vbuf[at, :].astype(jnp.bfloat16)
-        loop(0, X0R // CH, convert)
-        if c == 0:
-            pl.semaphore_wait(barrier, 7)
-        x0_copy(mine, c, 0).start()
-        if c < RING:
-            a_copy(jnp.int32(c)).start()
-    for c in range(X0C):
-        x0_copy(mine, c, 1).start()
+        x_in(c, 1).start()
+    for n in range(1, RING):
+        a_copy(jnp.int32(n)).start()
+
+    def take_x(h):
+        for c in range(X0C):
+            x_in(c, h).wait()
+
+            def convert(i, c=c):
+                at = rows_of(mine + c * X0R + i * CH, CH)
+                xbf[at, cols(h)] = vbuf[at, cols(h)].astype(jnp.bfloat16)
+            loop(0, X0R // CH, convert)
+            if c == 0 and h == 0:
+                pl.semaphore_wait(barrier, 7)
+            x0_copy(mine, c, h).start()
+
+    def half_product(start):
+        at = rows_of(start, PIECE)
+        return jnp.dot(abuf[0, :, at], xbf[at, cols(0)], preferred_element_type=jnp.float32)
+
+    take_x(0)
+    a_copy(jnp.int32(0)).wait()
+    first = rows_of(block_of(jnp.int32(0)), BR)
+    ybuf[first, cols(0)] = half_product(mine)
+    take_x(1)
+    x0_copy(far, 0, 0, X0C).wait_recv()
+    ybuf[first, cols(0)] = ybuf[first, cols(0)] + half_product(far)
+
+    @pl.when(home)
+    def _():
+        c_a(jnp.int32(0), 0).start()
+
+    @pl.when(away)
+    def _():
+        c_gy(jnp.int32(0), 0).start()
     d_in.start()
 
     @pl.when(away)
@@ -214,17 +238,18 @@
             return acc + fold(vbuf[rows_of(at, CH), :] * flags(at, None))
         s0buf[row] = lax.fori_loop(0, PIECE // CH, add, jnp.zeros((8, VECS), jnp.float32))
 
+    def new_x(at, own, there, h, one, two):
+        y = (ybuf[rows_of(at, CH), cols(h)] + one[there, cols(h)]) + two[there, cols(h)]
+        cf = jnp.concatenate([coef[:, cols(h)]] * (CH // 8), axis=0)
+        return DAMPING * y + cf * vbuf[rows_of(own, CH), cols(h)]
+
     def update(t, b, h, one, two, acc):
         def step(c, acc):
-            at = rows_of(same + t * PIECE + b * BR + c * CH, CH)
-            own = rows_of(t * PIECE + b * BR + c * CH, CH)
-            there = rows_of(b * BR + c * CH, CH)
-            y = (ybuf[at, cols(h)] + one[there, cols(h)]) + two[there, cols(h)]
-            cf = jnp.concatenate([coef[:, cols(h)]] * (CH // 8), axis=0)
-            x = DAMPING * y + cf * vbuf[own, cols(h)]
-            xbf[own, cols(h)] = x.astype(jnp.bfloat16)
-            ybuf[at, cols(h)] = x
-            return acc + fold(x * flags(t * PIECE + b * BR + c * CH, h))
+            own = t * PIECE + b * BR + c * CH
+            x = new_x(same + own, own, rows_of(b * BR + c * CH, CH), h, one, two)
+            xbf[rows_of(own, CH), cols(h)] = x.astype(jnp.bfloat16)
+            ybuf[rows_of(same + own, CH), cols(h)] = x
+            return acc + fold(x * flags(own, h))
         return lax.fori_loop(0, BR // CH, step, acc)
 
     def keep(t, b, h):
@@ -284,8 +309,13 @@
                 for h in range(2):
                     arrived(c_fy if kept == 0 else c_fx, end, h)
                 (held_a() if kept == 0 else held_dy()).wait_recv()
-                for h in range(2):
-                    result(kept, end, h)
+                one, two = (ra, rfy) if kept == 0 else (rdy, rfx)
+
+                def last_rows(c):
+                    own = kept * PIECE + (NB - 1) * BR + c * CH
+                    there = rows_of((NB - 1) * BR + c * CH, CH)
+                    out[there, :] = new_x(same + own, own, there, None, one, two)
+                loop(0, BR // CH, last_rows)
 
     def drain_forward():
         @pl.when(home)
@@ -314,7 +344,7 @@
                 a_copy(lax.rem(n, 4 * NB)).start()
 
         def lead(h):
-            def one(n):
+            def block(n):
                 if h == 0:
                     a_copy(n).wait()
                 multiply(n, h)
@@ -328,11 +358,12 @@
                 @pl.when(away)
                 def _():
                     c_gy(n, h).start()
-            loop(0, G, one)
-
-        @pl.when(k == 0)
-        def _():
-            x0_copy(far, 0, 0, X0C).wait_recv()
+
+            def one(n):
+                @pl.when(jnp.logical_or(k > 0, n > 0))
+                def _():
+                    block(n)
+            loop(0, G, one if h == 0 else block)
 
         @pl.when(k > 0)
         def _():
@@ -579,7 +610,7 @@
                 pltpu.VMEM((2, 8, VECS), jnp.float32),
                 pltpu.VMEM((8, VECS), jnp.float32),
                 pltpu.VMEM((8, VECS), jnp.float32),
-                dma((RING,)), dma((X0C,)), dma, dma((2,)),
+                dma((RING,)), dma((2 * X0C,)), dma, dma((2,)),
                 dma, dma((NB // G,)), dma, dma((NB // G,)), dma, dma, dma, dma((E // G + 4,)), dma, dma((E // G + 4,)),
                 dma, dma((2,)), dma, dma((2,)), dma, dma, dma, reg, reg, reg,
             ],

time: 821 us -> 822 us (level)
  no operation moved by 1% of the time
where the time goes in v17:
time: 822 us
  Pallas kernels  820 us (100%)
    pallas_call x1, Pallas kernels, local_sweeps(): pl.pallas_call(kernel, name='sweeps', out_shape=jax.ShapeDtypeStruct((PIE...  820 us

profile of v17, /device:TPU:0, one launch (start us, length us, event | category | flops | bytes accessed | tf_op | source)
XLA Modules:
  0.0 822.1 jit_solution(12560212492602639492)
XLA Ops:
  0.0 820.4 %sweeps.1 = f32[3072,256]{1,0:T(8,128)S(1)} custom-call(bf16[12288,6144]{1,0:T(8,128)(2,1)} %a_hbm.1, f32[3072,256]{1,0:T(8,128)} %x_hbm.1, f32[3072,256]{1,0:T(8,128)} %v_hbm.1, s32[24,128]{1,0:T(8,128)} %bitcast.1), custom_call_target="tpu_custom_call" | custom-call | flops 309237645312 | bytes 1207959552 | tf_op jit(solution)/shard_map/sweeps/pallas_call | solution.py:595
  820.4 1.7 copy.6

commit v18 on v17

--- a/solution.py
+++ b/solution.py
@@ -186,7 +186,6 @@
     a_copy(jnp.int32(0)).wait()
     first = rows_of(block_of(jnp.int32(0)), BR)
     ybuf[first, cols(0)] = half_product(mine)
-    take_x(1)
     x0_copy(far, 0, 0, X0C).wait_recv()
     ybuf[first, cols(0)] = ybuf[first, cols(0)] + half_product(far)
 
@@ -197,6 +196,7 @@
     @pl.when(away)
     def _():
         c_gy(jnp.int32(0), 0).start()
+    take_x(1)
     d_in.start()
 
     @pl.when(away)

time: 822 us -> 821 us (level)
  no operation moved by 1% of the time
where the time goes in v18:
time: 821 us
  Pallas kernels  819 us (100%)
    pallas_call x1, Pallas kernels, local_sweeps(): pl.pallas_call(kernel, name='sweeps', out_shape=jax.ShapeDtypeStruct((PIE...  819 us

profile of v18, /device:TPU:0, one launch (start us, length us, event | category | flops | bytes accessed | tf_op | source)
XLA Modules:
  0.0 821.2 jit_solution(843157512038262174)
XLA Ops:
  0.0 819.5 %sweeps.1 = f32[3072,256]{1,0:T(8,128)S(1)} custom-call(bf16[12288,6144]{1,0:T(8,128)(2,1)} %a_hbm.1, f32[3072,256]{1,0:T(8,128)} %x_hbm.1, f32[3072,256]{1,0:T(8,128)} %v_hbm.1, s32[24,128]{1,0:T(8,128)} %bitcast.1), custom_call_target="tpu_custom_call" | custom-call | flops 309237645312 | bytes 1207959552 | tf_op jit(solution)/shard_map/sweeps/pallas_call | solution.py:595
  819.5 1.7 copy.6

commit v19 on v16

--- a/solution.py
+++ b/solution.py
@@ -214,17 +214,18 @@
             return acc + fold(vbuf[rows_of(at, CH), :] * flags(at, None))
         s0buf[row] = lax.fori_loop(0, PIECE // CH, add, jnp.zeros((8, VECS), jnp.float32))
 
+    def new_x(at, own, there, h, one, two):
+        y = (ybuf[rows_of(at, CH), cols(h)] + one[there, cols(h)]) + two[there, cols(h)]
+        cf = jnp.concatenate([coef[:, cols(h)]] * (CH // 8), axis=0)
+        return DAMPING * y + cf * vbuf[rows_of(own, CH), cols(h)]
+
     def update(t, b, h, one, two, acc):
         def step(c, acc):
-            at = rows_of(same + t * PIECE + b * BR + c * CH, CH)
-            own = rows_of(t * PIECE + b * BR + c * CH, CH)
-            there = rows_of(b * BR + c * CH, CH)
-            y = (ybuf[at, cols(h)] + one[there, cols(h)]) + two[there, cols(h)]
-            cf = jnp.concatenate([coef[:, cols(h)]] * (CH // 8), axis=0)
-            x = DAMPING * y + cf * vbuf[own, cols(h)]
-            xbf[own, cols(h)] = x.astype(jnp.bfloat16)
-            ybuf[at, cols(h)] = x
-            return acc + fold(x * flags(t * PIECE + b * BR + c * CH, h))
+            own = t * PIECE + b * BR + c * CH
+            x = new_x(same + own, own, rows_of(b * BR + c * CH, CH), h, one, two)
+            xbf[rows_of(own, CH), cols(h)] = x.astype(jnp.bfloat16)
+            ybuf[rows_of(same + own, CH), cols(h)] = x
+            return acc + fold(x * flags(own, h))
         return lax.fori_loop(0, BR // CH, step, acc)
 
     def keep(t, b, h):
@@ -284,8 +285,13 @@
                 for h in range(2):
                     arrived(c_fy if kept == 0 else c_fx, end, h)
                 (held_a() if kept == 0 else held_dy()).wait_recv()
-                for h in range(2):
-                    result(kept, end, h)
+                one, two = (ra, rfy) if kept == 0 else (rdy, rfx)
+
+                def last_rows(c):
+                    own = kept * PIECE + (NB - 1) * BR + c * CH
+                    there = rows_of((NB - 1) * BR + c * CH, CH)
+                    out[there, :] = new_x(same + own, own, there, None, one, two)
+                loop(0, BR // CH, last_rows)
 
     def drain_forward():
         @pl.when(home)

time: 821 us -> 821 us (level)
  no operation moved by 1% of the time
where the time goes in v19:
time: 821 us
  Pallas kernels  819 us (100%)
    pallas_call x1, Pallas kernels, local_sweeps(): pl.pallas_call(kernel, name='sweeps', out_shape=jax.ShapeDtypeStruct((PIE...  819 us

profile of v19, /device:TPU:0, one launch (start us, length us, event | category | flops | bytes accessed | tf_op | source)
XLA Modules:
  0.0 821.1 jit_solution(10767127465577547415)
XLA Ops:
  0.0 819.4 %sweeps.1 = f32[3072,256]{1,0:T(8,128)S(1)} custom-call(bf16[12288,6144]{1,0:T(8,128)(2,1)} %a_hbm.1, f32[3072,256]{1,0:T(8,128)} %x_hbm.1, f32[3072,256]{1,0:T(8,128)} %v_hbm.1, s32[24,128]{1,0:T(8,128)} %bitcast.1), custom_call_target="tpu_custom_call" | custom-call | flops 309237645312 | bytes 1207959552 | tf_op jit(solution)/shard_map/sweeps/pallas_call | solution.py:570
  819.4 1.7 copy.6

commit v20 on v18

--- a/solution.py
+++ b/solution.py
@@ -301,11 +301,8 @@
             def _():
                 end = jnp.int32(NB - 1)
                 for h in range(2):
-                    def both(b):
-                        piece(1 - kept, b, h)
-                        piece(kept, b, h)
-                    loop(E, NB - 1, both)
-                    piece(1 - kept, end, h)
+                    loop(E, NB, lambda b: piece(1 - kept, b, h))
+                    loop(E, NB - 1, lambda b: piece(kept, b, h))
                 for h in range(2):
                     arrived(c_fy if kept == 0 else c_fx, end, h)
                 (held_a() if kept == 0 else held_dy()).wait_recv()

time: 821 us -> 821 us (level)
  no operation moved by 1% of the time
where the time goes in v20:
time: 821 us
  Pallas kernels  819 us (100%)
    pallas_call x1, Pallas kernels, local_sweeps(): pl.pallas_call(kernel, name='sweeps', out_shape=jax.ShapeDtypeStruct((PIE...  819 us

profile of v20, /device:TPU:0, one launch (start us, length us, event | category | flops | bytes accessed | tf_op | source)
XLA Modules:
  0.0 820.9 jit_solution(12234998512796607238)
XLA Ops:
  0.0 819.2 %sweeps.1 = f32[3072,256]{1,0:T(8,128)S(1)} custom-call(bf16[12288,6144]{1,0:T(8,128)(2,1)} %a_hbm.1, f32[3072,256]{1,0:T(8,128)} %x_hbm.1, f32[3072,256]{1,0:T(8,128)} %v_hbm.1, s32[24,128]{1,0:T(8,128)} %bitcast.1), custom_call_target="tpu_custom_call" | custom-call | flops 309237645312 | bytes 1207959552 | tf_op jit(solution)/shard_map/sweeps/pallas_call | solution.py:592
  819.2 1.7 copy.6

commit v21 on v20

--- a/solution.py
+++ b/solution.py
@@ -189,13 +189,20 @@
     x0_copy(far, 0, 0, X0C).wait_recv()
     ybuf[first, cols(0)] = ybuf[first, cols(0)] + half_product(far)
 
-    @pl.when(home)
-    def _():
-        c_a(jnp.int32(0), 0).start()
-
-    @pl.when(away)
-    def _():
-        c_gy(jnp.int32(0), 0).start()
+    def send_lead(n, h):
+        @pl.when(home)
+        def _():
+            c_a(n, h).start()
+
+        @pl.when(away)
+        def _():
+            c_gy(n, h).start()
+
+    send_lead(jnp.int32(0), 0)
+    a_copy(jnp.int32(1)).wait()
+    ybuf[rows_of(block_of(jnp.int32(1)), BR), cols(0)] = jnp.dot(
+        abuf[1], xbf[:, cols(0)], preferred_element_type=jnp.float32)
+    send_lead(jnp.int32(1), 0)
     take_x(1)
     d_in.start()
 
@@ -348,16 +355,10 @@
                 if h == 1:
                     fetch(n + RING)
 
-                @pl.when(home)
-                def _():
-                    c_a(n, h).start()
-
-                @pl.when(away)
-                def _():
-                    c_gy(n, h).start()
+                send_lead(n, h)
 
             def one(n):
-                @pl.when(jnp.logical_or(k > 0, n > 0))
+                @pl.when(jnp.logical_or(k > 0, n > 1))
                 def _():
                     block(n)
             loop(0, G, one if h == 0 else block)

time: 821 us -> 821 us (level)
  no operation moved by 1% of the time
where the time goes in v21:
time: 821 us; the launch traced here: 820 us
  Pallas kernels  819 us (100%)
    pallas_call x1, Pallas kernels, local_sweeps(): pl.pallas_call(kernel, name='sweeps', out_shape=jax.ShapeDtypeStruct((PIE...  819 us

profile of v21, /device:TPU:0, one launch (start us, length us, event | category | flops | bytes accessed | tf_op | source)
XLA Modules:
  0.0 820.4 jit_solution(5558971049630595574)
XLA Ops:
  0.0 818.8 %sweeps.1 = f32[3072,256]{1,0:T(8,128)S(1)} custom-call(bf16[12288,6144]{1,0:T(8,128)(2,1)} %a_hbm.1, f32[3072,256]{1,0:T(8,128)} %x_hbm.1, f32[3072,256]{1,0:T(8,128)} %v_hbm.1, s32[24,128]{1,0:T(8,128)} %bitcast.1), custom_call_target="tpu_custom_call" | custom-call | flops 309237645312 | bytes 1207959552 | tf_op jit(solution)/shard_map/sweeps/pallas_call | solution.py:593
  818.8 1.7 copy.6

commit v22 on v21

--- a/solution.py
+++ b/solution.py
@@ -171,9 +171,9 @@
             x_in(c, h).wait()
 
             def convert(i, c=c):
-                at = rows_of(mine + c * X0R + i * CH, CH)
+                at = rows_of(mine + c * X0R + i * HALF, HALF)
                 xbf[at, cols(h)] = vbuf[at, cols(h)].astype(jnp.bfloat16)
-            loop(0, X0R // CH, convert)
+            loop(0, X0R // HALF, convert)
             if c == 0 and h == 0:
                 pl.semaphore_wait(barrier, 7)
             x0_copy(mine, c, h).start()

time: 821 us -> 820 us (level)
  no operation moved by 1% of the time
where the time goes in v22:
time: 820 us
  Pallas kernels  819 us (100%)
    pallas_call x1, Pallas kernels, local_sweeps(): pl.pallas_call(kernel, name='sweeps', out_shape=jax.ShapeDtypeStruct((PIE...  819 us

profile of v22, /device:TPU:0, one launch (start us, length us, event | category | flops | bytes accessed | tf_op | source)
XLA Modules:
  0.0 820.3 jit_solution(16724484646328824835)
XLA Ops:
  0.0 818.7 %sweeps.1 = f32[3072,256]{1,0:T(8,128)S(1)} custom-call(bf16[12288,6144]{1,0:T(8,128)(2,1)} %a_hbm.1, f32[3072,256]{1,0:T(8,128)} %x_hbm.1, f32[3072,256]{1,0:T(8,128)} %v_hbm.1, s32[24,128]{1,0:T(8,128)} %bitcast.1), custom_call_target="tpu_custom_call" | custom-call | flops 309237645312 | bytes 1207959552 | tf_op jit(solution)/shard_map/sweeps/pallas_call | solution.py:593
  818.7 1.7 copy.6
